TPU v7x, 256 devices: a 4x2x16 block of a 4x16x16 slice. The times are simulated.
256 devices in a mesh: groups: 2 (over y), dp: 2 (over core), tensor: 64 (over x, z).
Axes of the slice: x: 4, y: 2, z: 16, core: 2. Of those that a mesh axis runs over, the one named last changes fastest.
The devices are a block of a 4x16x16 slice.
Arguments:
- hidden_in: bfloat16 [4, 1024, 5120], P(('groups', 'dp'), 'tensor'), parts along dimension 0, may hold values from -40 to 40
- first_values: bfloat16 [4, 1024, 8192], P(('groups', 'dp'), 'tensor'), parts along dimension 0, may hold values from -6 to 6
- qkv_weight: bfloat16 [5120, 3, 8192], P(None, None, 'tensor'), may hold values from -1 to 1
- out_weight: bfloat16 [8192, 5120], P('tensor'), may hold values from -0.1875 to 0.1875
- mix_table: float32 [8, 2], replicated, may hold values from 0.2 to 1
- mix_index: int32 [64], P('tensor'), may hold values from 0 to 7
- lengths: int32 [4], P(('groups', 'dp')), parts along dimension 0, may hold values from 256 to 1024
Outputs:
- attn_out: bfloat16 [4, 1024, 5120], P(('groups', 'dp'), 'tensor'), parts along dimension 0
There are 2 independent parts, one for each index of `groups`. A program takes and returns all parts, laid end to end along the dimension named above; an argument that names none is the same for every part. Nothing has to cross between parts.
All inputs are finite; a program needn't handle non-finite values.
Results may differ from a plain program's by a relative error of at most 0.0077.
Values may be sent and summed in bfloat16 or wider, within the bound.
A program may use at most 128 MiB of HBM per device.

v0:
```python
import math

import jax
import jax.numpy as jnp
from jax import lax
from jax.sharding import Mesh
from jax.sharding import PartitionSpec as P

TENSOR = ("tensor_0", "tensor_1")


NEG_FILL = -1e30


def summed_rows(subtotal, axes):
    for axis in axes:
        subtotal = lax.psum_scatter(subtotal, axis, scatter_dimension=0, tiled=True)
    return subtotal


def body(hidden_in, first_values, qkv_weight, out_weight, mix_table, mix_index, lengths):
    local_rows = hidden_in[0]
    model_width = local_rows.shape[1]
    head_width = qkv_weight.shape[2]
    heads_here = mix_index.shape[0]
    head_size = head_width // heads_here
    merged_weight = qkv_weight.reshape(model_width, 3 * head_width)
    projected = jnp.dot(
        lax.all_gather(local_rows, TENSOR, axis=0, tiled=True),
        merged_weight,
        preferred_element_type=jnp.float32,
    ).astype(jnp.bfloat16)
    relaid = lax.all_to_all(first_values[0], TENSOR, split_axis=1, concat_axis=0, tiled=True)
    total_rows = projected.shape[0]
    split_parts = projected.reshape(total_rows, 3, heads_here, head_size)
    queries = split_parts[:, 0]
    key_rows = split_parts[:, 1]
    firsts = relaid.reshape(total_rows, heads_here, head_size)
    levels = mix_table.shape[0]
    one_hot = (mix_index[:, None] == jnp.arange(levels, dtype=jnp.int32)[None, :]).astype(
        jnp.float32
    )
    weights_mix = jnp.dot(one_hot, mix_table, precision=lax.Precision.HIGHEST)
    mixed_values = (
        weights_mix[None, :, 0:1] * split_parts[:, 2].astype(jnp.float32)
        + weights_mix[None, :, 1:2] * firsts.astype(jnp.float32)
    ).astype(jnp.bfloat16)
    positions = jnp.arange(total_rows, dtype=jnp.int32)
    valid_length = lengths[0]
    score_scale = 1.0 / math.sqrt(head_size)
    block_rows = min(512, total_rows)

    def attend(first_row):
        query_block = lax.dynamic_slice_in_dim(queries, first_row, block_rows, 0)
        row_positions = first_row + jnp.arange(block_rows, dtype=jnp.int32)
        scores = (
            jnp.einsum("qhd,khd->hqk", query_block, key_rows, preferred_element_type=jnp.float32)
            * score_scale
        )
        allowed = (positions[None, :] <= row_positions[:, None]) & (
            positions[None, :] < valid_length
        )
        scores = jnp.where(allowed[None], scores, NEG_FILL)
        row_max = jnp.max(scores, axis=2, keepdims=True)
        raised = jnp.exp(scores - row_max)
        weights = (raised / jnp.sum(raised, axis=2, keepdims=True)).astype(jnp.bfloat16)
        return jnp.einsum(
            "hqk,khd->qhd", weights, mixed_values, preferred_element_type=jnp.float32
        ).astype(jnp.bfloat16)

    starts = jnp.arange(total_rows // block_rows, dtype=jnp.int32) * block_rows
    outputs = lax.map(attend, starts).reshape(total_rows, head_width)
    kept_rows = summed_rows(
        jnp.dot(outputs, out_weight, preferred_element_type=jnp.float32), TENSOR
    )
    return kept_rows.astype(jnp.bfloat16)[None]


def solution(mesh):
    torus = Mesh(
        mesh.devices.reshape(mesh.shape["groups"], mesh.shape["dp"], 4, 16),
        ("groups", "dp", "tensor_0", "tensor_1"),
    )
    placed = (
        P(("groups", "dp"), TENSOR, None),
        P(("groups", "dp"), TENSOR, None),
        P(None, None, TENSOR),
        P(TENSOR, None),
        P(),
        P(TENSOR),
        P(("groups", "dp")),
    )
    return jax.shard_map(
        body,
        mesh=torus,
        in_specs=placed,
        out_specs=P(("groups", "dp"), TENSOR, None),
        check_vma=False,
    )
```

profile of v0, /device:TPU:40, one launch (start us, length us, event | category | flops | bytes accessed | tf_op | source)
XLA Modules:
  0.0 489.5 jit_solution(7217374364161948527)
XLA Ops:
  6.5 0.0 copy-start
  6.6 0.0 all-gather.3.cloned.1.call-start
  6.6 0.7 all-gather.3.cloned.1.call-update
  7.3 1.0 copy.20
  8.3 0.9 copy.16
  9.2 29.0 %all-to-all-start = ((bf16[16,64,128]{2,0,1:T(8,128)(2,1)}), bf16[16,64,128]{2,0,1:T(8,128)(2,1)S(1)}, u32[]{:S(2)}, u32[]{:S(2)}) async-start(bf16[16,64,128]{2,0,1:T(8,128)(2,1)} %copy.16), calls=%async_computation | async-start | bytes 524288 | tf_op jit(solution)/shard_map/all_to_all | solution.py:33
  38.2 0.1 reduce-scatter.3.cloned.1.call-start
  39.0 0.0 copy-start.1
  39.0 6.3 %copy.12 = bf16[5120,3,128]{0,2,1:T(8,128)(2,1)} copy(bf16[5120,3,128]{2,0,1:T(8,128)(2,1)} %param.11) | data formatting | bytes 7864320 | tf_op args[2]
  45.3 0.0 copy-done.1
  45.3 0.1 fusion.17
  45.4 0.6 fusion.22
  46.1 14.2 %all-to-all-done = bf16[16,64,128]{2,0,1:T(8,128)(2,1)S(1)} async-done(((bf16[16,64,128]{2,0,1:T(8,128)(2,1)}), bf16[16,64,128]{2,0,1:T(8,128)(2,1)S(1)}, u32[]{:S(2)}, u32[]{:S(2)}) %all-to-all-start) | async-done | bytes 262176 | tf_op jit(solution)/shard_map/all_to_all | solution.py:33
  60.3 0.7 convert_multiply_fusion
  60.9 123.3 %all-gather.3.cloned.1.call-done = bf16[1,1024,5120]{2,1,0:T(8,128)(2,1)} async-done(((bf16[1,16,5120]{2,1,0:T(8,128)(2,1)}), bf16[1,1024,5120]{2,1,0:T(8,128)(2,1)}) %all-gather.3.cloned.1.call-update) | async-done | bytes 10485776 | tf_op jit(solution)/shard_map/all_gather | solution.py:29
  184.2 9.3 %fusion.13 = bf16[1024,384]{0,1:T(8,128)(2,1)S(1)} fusion(bf16[5120,384]{0,1:T(8,128)(2,1)} %bitcast.71, bf16[1,1024,5120]{2,1,0:T(8,128)(2,1)} %all-gather.3.cloned.1.call-done), kind=kOutput, calls=%fused_computation.19 | convolution fusion | flops 4026925056 | bytes 15204352 | tf_op jit(solution)/shard_map/dot_general | solution.py:28
  193.6 0.1 fusion.21
  193.6 0.2 copy.19
  193.8 0.2 copy.18
  194.0 0.2 copy.17
  194.2 0.7 fusion.16
  194.9 10.8 %while.12 = (s32[]{:T(128)}, bf16[2,512,1,128]{3,1,2,0:T(8,128)(2,1)S(1)}, s32[2]{0:T(128)S(1)}, s32[]{:T(128)}, bf16[1024,1,128]{2,0,1:T(8,128)(2,1)S(1)}, /*in...) while((s32[]{:T(128)}, ...), condition=%wide.region_3.4_spmd.clone.clone, body=%wide.region_0.3_spmd.clone.clone.sunk | while | flops 273744384 | bytes 7094443 | solution.py:72
  194.9 0.6 dynamic_slice.20
  197.2 0.7 iota_compare_fusion.3
  197.9 0.6 iota_add_fusion.2
  198.4 0.8 fusion.33
  199.2 0.5 fusion.34
  199.7 0.6 fusion.35
  200.3 0.6 dynamic_slice.20
  202.6 0.7 iota_compare_fusion.3
  203.3 0.6 iota_add_fusion.2
  203.8 0.8 fusion.33
  204.6 0.5 fusion.34
  205.1 0.6 fusion.35
  205.7 0.0 copy-done
  205.8 8.6 %fusion.23 = f32[1024,5120]{1,0:T(8,128)} fusion(bf16[1024,128]{1,0:T(8,128)(2,1)S(1)} %bitcast.75, bf16[128,5120]{1,0:T(8,128)(2,1)S(1)} %copy-done), kind=kOutput, calls=%fused_computation.32 | convolution fusion | flops 1342177280 | bytes 22544384 | tf_op jit(solution)/shard_map/dot_general | solution.py:74
  214.3 0.1 reduce-scatter.3.cloned.1.call-update
  214.4 0.1 reduce-scatter.5.cloned.1.call-start
  214.5 182.7 %reduce-scatter.3.cloned.1.call-done = f32[256,5120]{1,0:T(8,128)} async-done(((f32[1024,5120]{1,0:T(8,128)}), f32[256,5120]{1,0:T(8,128)}) %reduce-scatter.3.cloned.1.call-update) | async-done | bytes 5242896 | tf_op jit(solution)/shard_map/reduce_scatter | solution.py:17
  397.1 0.1 reduce-scatter.5.cloned.1.call-update
  397.2 84.1 %reduce-scatter.5.cloned.1.call-done = f32[16,5120]{1,0:T(8,128)} async-done(((f32[256,5120]{1,0:T(8,128)}), f32[16,5120]{1,0:T(8,128)}) %reduce-scatter.5.cloned.1.call-update) | async-done | bytes 327696 | tf_op jit(solution)/shard_map/reduce_scatter | solution.py:17
  481.3 1.7 convert_bitcast_fusion
  (2 shorter events, 0.0 us)
Async XLA Ops:
  6.5 199.2 %copy-start = (bf16[128,5120]{1,0:T(8,128)(2,1)S(1)}, bf16[128,5120]{1,0:T(8,128)(2,1)}, u32[]{:S(2)}) copy-start(bf16[128,5120]{1,0:T(8,128)(2,1)} %param.12) | copy-start | bytes 3932164
  6.6 177.7 %all-gather.3.cloned.1.call-start = ((), (), s32[]{:S(2)}) async-start(), calls=%async_computation.5 | async-start | bytes 10649600 | tf_op jit(solution)/shard_map/all_gather | solution.py:29
  9.2 51.1 %all-to-all-start = ((bf16[16,64,128]{2,0,1:T(8,128)(2,1)}), bf16[16,64,128]{2,0,1:T(8,128)(2,1)S(1)}, u32[]{:S(2)}, u32[]{:S(2)}) async-start(bf16[16,64,128]{2,0,1:T(8,128)(2,1)} %copy.16), calls=%async_computation | async-start | bytes 524288 | tf_op jit(solution)/shard_map/all_to_all | solution.py:33
  38.2 358.9 %reduce-scatter.3.cloned.1.call-start = ((), (), s32[]{:S(2)}) async-start(), calls=%async_computation.3 | async-start | bytes 26214400 | tf_op jit(solution)/shard_map/reduce_scatter | solution.py:17
  39.0 6.4 %copy-start.1 = (f32[8,2]{0,1:T(2,128)S(1)}, f32[8,2]{0,1:T(2,128)}, u32[]{:S(2)}) copy-start(f32[8,2]{0,1:T(2,128)} %param.13) | copy-start | bytes 196
  214.4 266.9 %reduce-scatter.5.cloned.1.call-start = ((), (), s32[]{:S(2)}) async-start(), calls=%async_computation.4 | async-start | bytes 5570560 | tf_op jit(solution)/shard_map/reduce_scatter | solution.py:17
Sparse Core Ops, SparseCore 0:
  9.8 174.4 all-gather.2
  214.5 182.5 reduce-scatter.2
  399.7 81.5 reduce-scatter.4
where the time goes:
time: 490 us; the launch traced here: 489 us
  waiting for transfers between devices  405 us (83%)
  starting transfers between devices  29.2 us (6%)
  matrix products  20.8 us (4%)
  between operations  13.9 us (3%)
  local copies, waits for them, and re-layouts  10.6 us (2%)
  other arithmetic  6.53 us (1%)
    reduce_scatter x2, waiting for transfers between devices, summed_rows(): subtotal = lax.psum_scatter(subtotal, axis, scatter_dimension=0, tiled=True)  267 us
    all_gather x1, waiting for transfers between devices, body(): lax.all_gather(local_rows, TENSOR, axis=0, tiled=True)  123 us
    all_to_all x1, starting transfers between devices, body(): lax.all_to_all(first_values[0], TENSOR, split_axis=1, concat_axis=0, tile...  29 us
    all_to_all x1, waiting for transfers between devices, body(): lax.all_to_all(first_values[0], TENSOR, split_axis=1, concat_axis=0, tile...  14.2 us
  transfers between devices with their start and end apart: 4, of which 4 were waited for; matrix products, arithmetic and copies ran while one was open for 2% of the time, Pallas kernels for 0%

commit v1 on v0

v1 whole, which is shorter than its diff:
```python
import functools
import math

import jax
import jax.numpy as jnp
from jax import lax
from jax.experimental import pallas as pl
from jax.experimental.pallas import tpu as pltpu
from jax.sharding import Mesh
from jax.sharding import PartitionSpec as P

TENSOR = ("tensor_0", "tensor_1")
NEG_FILL = -1e30
BF = jnp.bfloat16
F32 = jnp.float32
NX = 4
SUB = 256
LAG = 2


def kernel(
    nz,
    hid,
    firsts,
    w_qkv,
    w_out,
    mix_table,
    mix_index,
    lengths,
    out,
    h_buf,
    w2,
    w_relay,
    wo2,
    wo_relay,
    fv_stage,
    fv_own,
    fv_plus,
    fv_minus,
    stash,
    a_send,
    a_recv,
    b_send,
    b_recv,
    q_buf,
    k_buf,
    v_buf,
    att,
    rs_send,
    rs_recv,
    fin,
    out_v,
    local_sem,
    send_sem,
    hid_sem,
    ag_sem,
    w_sem,
    wo_sem,
    fx_sem,
    fz_sem,
    a_sem,
    b_sem,
    att_sem,
    rs_sem,
    fin_sem,
):
    rows, model = hid.shape
    hs = w_qkv.shape[2]
    quarter = model // NX
    half = quarter // 2
    subs = quarter // SUB
    turns = nz // 2
    block = NX * rows

    x = lax.axis_index("tensor_0")
    z = lax.axis_index("tensor_1")
    core = lax.axis_index("dp")
    xs = [x] + [lax.rem(x + d, NX) for d in range(1, NX)]
    z_up = lax.rem(z + 1, nz)
    z_down = lax.rem(z + nz - 1, nz)
    x_way = lax.rem(x + 1 + 2 * core, NX)

    def remote(src, dst, send, recv, **where):
        return pltpu.make_async_remote_copy(
            src_ref=src,
            dst_ref=dst,
            send_sem=send,
            recv_sem=recv,
            device_id=where,
            device_id_type=pl.DeviceIdType.MESH,
        )

    def arrived(ref, sem):
        pltpu.make_async_copy(ref, ref, sem).wait()

    barrier = pltpu.get_barrier_semaphore()
    partners = [
        {"dp": 1 - core},
        {"tensor_0": xs[1]},
        {"tensor_0": xs[2]},
        {"tensor_0": xs[3]},
        {"tensor_1": z_up},
        {"tensor_1": z_down},
    ]
    for partner in partners:
        pl.semaphore_signal(
            barrier, inc=1, device_id=partner, device_id_type=pl.DeviceIdType.MESH
        )
    pl.semaphore_wait(barrier, len(partners))

    for d in (1, 2, 3):
        for s in range(subs):
            column = pl.multiple_of(xs[d] * quarter + s * SUB, 128)
            remote(
                hid.at[:, pl.ds(column, SUB)],
                h_buf.at[0, s, x],
                send_sem.at[0],
                hid_sem.at[d, s],
                tensor_0=xs[d],
            ).start()
    own_hidden = []
    for s in range(subs):
        column = pl.multiple_of(x * quarter + s * SUB, 128)
        own_hidden.append(
            pltpu.make_async_copy(
                hid.at[:, pl.ds(column, SUB)], h_buf.at[0, s, x], hid_sem.at[0, s]
            )
        )
        own_hidden[-1].start()

    my_half = pl.multiple_of(core * half, 128)

    def w_rows(to):
        return pl.ds(pl.multiple_of(to * quarter + core * half, 128), half)

    for p in range(3):
        remote(
            w_qkv.at[p, w_rows(xs[2])],
            w_relay.at[p],
            send_sem.at[1],
            w_sem.at[0, p],
            tensor_0=x_way,
        ).start()
    for d, r, sem in ((1, 3, 1), (3, 1, 2)):
        for p in range(3):
            remote(
                w_qkv.at[p, w_rows(xs[d])],
                w2.at[pl.ds(my_half, half), pl.ds((r * 3 + p) * hs, hs)],
                send_sem.at[1],
                w_sem.at[sem, p],
                tensor_0=xs[d],
            ).start()
    own_weights = []
    for p in range(3):
        own_weights.append(
            pltpu.make_async_copy(
                w_qkv.at[p, pl.ds(pl.multiple_of(x * quarter, 128), quarter)],
                w2.at[:, pl.ds(p * hs, hs)],
                local_sem.at[p],
            )
        )
    own_weights.append(
        pltpu.make_async_copy(
            w_out.at[:, pl.ds(pl.multiple_of(x * quarter, 128), quarter)],
            wo2.at[pl.ds(0, hs)],
            local_sem.at[3],
        )
    )
    for copy in own_weights:
        copy.start()

    def stage_firsts(head, carry):
        away = lax.rem(head - z + nz, nz)
        for d in range(NX):
            column = pl.multiple_of((xs[d] * nz + head) * hs, 128)
            piece = firsts[:, pl.ds(column, hs)]
            if d == 0:
                fv_own[away, x] = piece
            else:
                fv_stage[d - 1, away] = piece
        return carry

    lax.fori_loop(0, nz, stage_firsts, 0)
    for d in (1, 2, 3):
        remote(
            fv_stage.at[d - 1],
            fv_own.at[:, x],
            send_sem.at[2],
            fx_sem.at[d],
            tensor_0=xs[d],
        ).start()

    def length_of(way, s):
        return turns if (s % 2 == 0) == (way == 0) else turns - 1

    def gather_send(step):
        for s in range(subs):
            if step <= length_of(0, s):
                remote(
                    h_buf.at[(nz - step + 1) % nz, s],
                    h_buf.at[nz - step, s],
                    send_sem.at[3],
                    ag_sem.at[0, step - 1, s],
                    tensor_1=z_up,
                ).start()
            if step <= length_of(1, s):
                remote(
                    h_buf.at[step - 1, s],
                    h_buf.at[step, s],
                    send_sem.at[3],
                    ag_sem.at[1, step - 1, s],
                    tensor_1=z_down,
                ).start()

    def gather_step(step):
        for s in range(subs):
            if step <= length_of(0, s):
                arrived(h_buf.at[nz - step, s], ag_sem.at[0, step - 1, s])
            if step <= length_of(1, s):
                arrived(h_buf.at[step, s], ag_sem.at[1, step - 1, s])
            if step + 1 <= length_of(0, s):
                remote(
                    h_buf.at[nz - step, s],
                    h_buf.at[nz - step - 1, s],
                    send_sem.at[3],
                    ag_sem.at[0, step, s],
                    tensor_1=z_up,
                ).start()
            if step + 1 <= length_of(1, s):
                remote(
                    h_buf.at[step, s],
                    h_buf.at[step + 1, s],
                    send_sem.at[3],
                    ag_sem.at[1, step, s],
                    tensor_1=z_down,
                ).start()

    def half_columns(r):
        return w2.at[pl.ds(my_half, half), pl.ds(r * 3 * hs, 3 * hs)]

    def to_sibling(r):
        remote(
            half_columns(r), half_columns(r), send_sem.at[4], w_sem.at[4, r - 1], dp=1 - core
        ).start()

    def w_piece(r, p):
        return w2.at[pl.ds(my_half, half), pl.ds((r * 3 + p) * hs, hs)]

    def weights_relay():
        for p in range(3):
            arrived(w_relay.at[p], w_sem.at[0, p])
            remote(
                w_relay.at[p], w_piece(2, p), send_sem.at[5], w_sem.at[3, p], tensor_0=x_way
            ).start()

    def weights_direct():
        for r, sem in ((3, 1), (1, 2)):
            for p in range(3):
                arrived(w_piece(r, p), w_sem.at[sem, p])
            to_sibling(r)

    def weights_last():
        for p in range(3):
            arrived(w_piece(2, p), w_sem.at[3, p])
        to_sibling(2)
        for r in (1, 2, 3):
            other = pl.multiple_of((1 - core) * half, 128)
            arrived(
                w2.at[pl.ds(other, half), pl.ds(r * 3 * hs, 3 * hs)], w_sem.at[4, r - 1]
            )
        for copy in own_weights:
            copy.wait()

    for d in (1, 2, 3):
        for s in range(subs):
            arrived(h_buf.at[0, s, xs[d]], hid_sem.at[d, s])
    for copy in own_hidden:
        copy.wait()
    gather_send(1)
    early = max(turns - 3, 0)
    for step in range(1, early + 1):
        gather_step(step)
        if step == 2:
            weights_relay()
        if step == 4:
            weights_direct()
    if early < 2:
        weights_relay()
    if early < 4:
        weights_direct()
    weights_last()

    minus_turns = turns - 1

    def plus_at(step):
        return sum(turns + 1 - u for u in range(1, step))

    def minus_at(step):
        return sum(minus_turns + 1 - u for u in range(1, step))

    def firsts_step(step):
        if step == 0:
            for d in (1, 2, 3):
                arrived(fv_stage.at[d - 1], fx_sem.at[d])
            plus_src = fv_own.at[pl.ds(1, turns)]
            minus_src = fv_own.at[pl.ds(nz - minus_turns, minus_turns)]
        else:
            n_plus = turns + 1 - step
            arrived(fv_plus.at[pl.ds(plus_at(step), n_plus)], fz_sem.at[0, step - 1])
            plus_src = fv_plus.at[pl.ds(plus_at(step) + 1, n_plus - 1)] if n_plus > 1 else None
            n_minus = minus_turns + 1 - step
            minus_src = None
            if n_minus >= 1:
                arrived(fv_minus.at[pl.ds(minus_at(step), n_minus)], fz_sem.at[1, step - 1])
                if n_minus > 1:
                    minus_src = fv_minus.at[pl.ds(minus_at(step), n_minus - 1)]
        if plus_src is not None:
            remote(
                plus_src,
                fv_plus.at[pl.ds(plus_at(step + 1), turns - step)],
                send_sem.at[6],
                fz_sem.at[0, step],
                tensor_1=z_up,
            ).start()
        if minus_src is not None:
            remote(
                minus_src,
                fv_minus.at[pl.ds(minus_at(step + 1), minus_turns - step)],
                send_sem.at[7],
                fz_sem.at[1, step],
                tensor_1=z_down,
            ).start()

    width = 3 * hs
    low, high = pl.ds(0, block // 2), pl.ds(block // 2, block // 2)

    def place_of(i):
        return jnp.where(i % 2 == 1, (i + 1) // 2, lax.rem(nz - i // 2, nz))

    def project(i):
        place = place_of(i)
        lhs = jnp.concatenate(
            [h_buf[place, s].reshape(block, SUB) for s in range(subs)], axis=1
        )
        for r in (2, 1, 3, 0):
            term = jnp.dot(
                lhs, w2[:, r * width : (r + 1) * width], preferred_element_type=F32
            )
            if r == 2:
                a_send[i] = term.astype(BF)
                remote(
                    a_send.at[i, low],
                    a_recv.at[i, low],
                    send_sem.at[8],
                    a_sem.at[0, i],
                    tensor_0=xs[1],
                ).start()
                remote(
                    a_send.at[i, high],
                    a_recv.at[i, high],
                    send_sem.at[8],
                    a_sem.at[1, i],
                    tensor_0=xs[3],
                ).start()
            else:
                stash[i, r % 3 if r < 3 else 2] = term

    def pass_on(i):
        arrived(a_recv.at[i, low], a_sem.at[0, i])
        b_send[i, 0, low] = (stash[i, 1, low] + a_recv[i, low].astype(F32)).astype(BF)
        b_send[i, 0, high] = stash[i, 1, high].astype(BF)
        remote(
            b_send.at[i, 0], b_recv.at[i, 0], send_sem.at[9], b_sem.at[0, i], tensor_0=xs[1]
        ).start()
        arrived(a_recv.at[i, high], a_sem.at[1, i])
        b_send[i, 1, low] = stash[i, 2, low].astype(BF)
        b_send[i, 1, high] = (stash[i, 2, high] + a_recv[i, high].astype(F32)).astype(BF)
        remote(
            b_send.at[i, 1], b_recv.at[i, 1], send_sem.at[9], b_sem.at[1, i], tensor_0=xs[3]
        ).start()

    def finish(i):
        arrived(b_recv.at[i, 0], b_sem.at[0, i])
        arrived(b_recv.at[i, 1], b_sem.at[1, i])
        total = stash[i, 0] + b_recv[i, 0].astype(F32) + b_recv[i, 1].astype(F32)
        total = total.astype(BF).reshape(NX, rows, width)
        origin = lax.rem(z + place_of(i), nz)
        q_buf[:, origin] = total[:, :, :hs]
        k_buf[:, origin] = total[:, :, hs : 2 * hs]
        v_buf[:, origin] = total[:, :, 2 * hs :]

    def wo_columns(to):
        return pl.ds(pl.multiple_of(to * quarter + core * half, 128), half)

    def wo_piece(r):
        return wo2.at[pl.ds(r * hs, hs), pl.ds(my_half, half)]

    def out_weights_send():
        remote(
            w_out.at[:, wo_columns(xs[2])], wo_relay, send_sem.at[10], wo_sem.at[0], tensor_0=x_way
        ).start()
        for d, r, sem in ((1, 3, 1), (3, 1, 2)):
            remote(
                w_out.at[:, wo_columns(xs[d])],
                wo_piece(r),
                send_sem.at[10],
                wo_sem.at[sem],
                tensor_0=xs[d],
            ).start()

    def out_to_sibling(r):
        remote(
            wo_piece(r), wo_piece(r), send_sem.at[11], wo_sem.at[3 + r], dp=1 - core
        ).start()

    def out_weights_relay():
        arrived(wo_relay, wo_sem.at[0])
        remote(wo_relay, wo_piece(2), send_sem.at[12], wo_sem.at[3], tensor_0=x_way).start()

    def out_weights_direct():
        for r, sem in ((3, 1), (1, 2)):
            arrived(wo_piece(r), wo_sem.at[sem])
            out_to_sibling(r)

    def out_weights_last():
        arrived(wo_piece(2), wo_sem.at[3])
        out_to_sibling(2)

    def out_weights_wait():
        other = pl.multiple_of((1 - core) * half, 128)
        for r in (1, 2, 3):
            arrived(wo2.at[pl.ds(r * hs, hs), pl.ds(other, half)], wo_sem.at[3 + r])

    trips = nz + 2 * LAG
    late = {}
    for step in range(early + 1, turns + 1):
        late.setdefault(2 * (step - early) - 1, []).append(functools.partial(gather_step, step))
    for step in range(turns + 1):
        if 2 * step + 2 < trips:
            late.setdefault(2 * step + 2, []).append(functools.partial(firsts_step, step))

    def trip(i, carry):
        for at, steps in late.items():

            @pl.when(i == at)
            def _(steps=steps):
                for step in steps:
                    step()

        @pl.when(i < nz)
        def _():
            project(i)

        @pl.when((i >= LAG) & (i < nz + LAG))
        def _():
            pass_on(i - LAG)

        @pl.when(i == nz + LAG)
        def _():
            out_weights_send()

        @pl.when(i >= 2 * LAG)
        def _():
            finish(i - 2 * LAG)

        return carry

    lax.fori_loop(0, trips, trip, 0)
    for step in range(turns + 1):
        if 2 * step + 2 >= trips:
            firsts_step(step)

    row = mix_index[0]
    weight_now = mix_table[row, 0]
    weight_first = mix_table[row, 1]

    def mix(origin, first):
        now = v_buf[:, origin].astype(F32)
        v_buf[:, origin] = (weight_now * now + weight_first * first.astype(F32)).astype(BF)

    mix(z, fv_own[0])
    for step in range(1, turns + 1):
        mix(lax.rem(z + nz - step, nz), fv_plus[plus_at(step)])
    for step in range(1, minus_turns + 1):
        mix(lax.rem(z + step, nz), fv_minus[minus_at(step) + minus_turns - step])

    scale = 1.0 / math.sqrt(hs)
    valid = lengths[0]
    stripe = nz * rows
    q_blocks = min(nz, 128 // rows)
    q_rows = q_blocks * rows

    def attend(b):
        n = (b + 1) * stripe
        keys = k_buf[0 : b + 1].reshape(n, hs)
        values = v_buf[0 : b + 1].reshape(n, hs)

        def one(t, carry):
            at = pl.ds(t * q_blocks, q_blocks)
            query = q_buf[b, at].reshape(q_rows, hs)
            scores = (
                lax.dot_general(query, keys, (((1,), (1,)), ((), ())), preferred_element_type=F32)
                * scale
            )
            col = lax.broadcasted_iota(jnp.int32, (q_rows, n), 1)
            line = b * stripe + t * q_rows + lax.broadcasted_iota(jnp.int32, (q_rows, n), 0)
            scores = jnp.where((col <= line) & (col < valid), scores, NEG_FILL)
            raised = jnp.exp(scores - jnp.max(scores, axis=1, keepdims=True))
            weights = (raised * (1.0 / jnp.sum(raised, axis=1, keepdims=True))).astype(BF)
            result = jnp.dot(weights, values, preferred_element_type=F32).astype(BF)
            att[0, at, b] = result.reshape(q_blocks, rows, hs)
            return carry

        lax.fori_loop(0, nz // q_blocks, one, 0)

    near, far = pl.ds(0, nz // 2), pl.ds(nz // 2, nz // 2)

    def att_send(b):
        remote(
            att.at[0, :, b], att.at[3, :, b], send_sem.at[13], att_sem.at[0, b], tensor_0=xs[1]
        ).start()
        remote(
            att.at[0, :, b], att.at[1, :, b], send_sem.at[14], att_sem.at[1, b], tensor_0=xs[3]
        ).start()

    def att_pass(b):
        arrived(att.at[3, :, b], att_sem.at[0, b])
        remote(
            att.at[3, near, b], att.at[2, near, b], send_sem.at[15], att_sem.at[2, b], tensor_0=xs[1]
        ).start()
        arrived(att.at[1, :, b], att_sem.at[1, b])
        remote(
            att.at[1, far, b], att.at[2, far, b], send_sem.at[16], att_sem.at[3, b], tensor_0=xs[3]
        ).start()

    attend(0)
    att_send(0)
    out_weights_relay()
    attend(1)
    att_send(1)
    att_pass(0)
    attend(2)
    att_send(2)
    att_pass(1)
    out_weights_direct()
    attend(3)
    att_send(3)
    att_pass(2)
    out_weights_last()
    rs_recv[:, 0] = jnp.zeros(rs_recv.shape[:1] + rs_recv.shape[2:], BF)
    att_pass(3)
    out_weights_wait()
    for b in range(NX):
        arrived(att.at[2, near, b], att_sem.at[2, b])
        arrived(att.at[2, far, b], att_sem.at[3, b])

    def heads_of(away):
        origin = lax.rem(z + away + nz, nz)
        return jnp.concatenate([att[r, origin].reshape(block, hs) for r in range(NX)], axis=1)

    def columns(s):
        return wo2[:, s * SUB : (s + 1) * SUB]

    def reduce_step(step, carry):
        for s in range(subs):
            for way in (0, 1):
                length = length_of(way, s)
                sign = 1 - 2 * way

                @pl.when(step <= length)
                def _(s=s, way=way, length=length, sign=sign):
                    lhs = heads_of(sign * (length - step + 1))
                    term = jnp.dot(lhs, columns(s), preferred_element_type=F32)

                    @pl.when(step > 1)
                    def _():
                        arrived(rs_recv.at[way, step - 1, s], rs_sem.at[way, step - 1, s])

                    term = term + rs_recv[way, step - 1, s].astype(F32)
                    rs_send[step - 1, way, s] = term.astype(BF)
                    remote(
                        rs_send.at[step - 1, way, s],
                        rs_recv.at[way, step, s],
                        send_sem.at[17],
                        rs_sem.at[way, step, s],
                        tensor_1=z_up if way == 0 else z_down,
                    ).start()

        return carry

    lax.fori_loop(1, turns + 1, reduce_step, 0)
    own = heads_of(0)
    for s in range(subs):
        term = jnp.dot(own, columns(s), preferred_element_type=F32)
        for way in (0, 1):
            length = length_of(way, s)
            arrived(rs_recv.at[way, length, s], rs_sem.at[way, length, s])
            term = term + rs_recv[way, length, s].astype(F32)
        fin[s] = term.astype(BF).reshape(NX, rows, SUB)
        column = pl.multiple_of(x * quarter + s * SUB, 128)
        for d in (1, 2, 3):
            remote(
                fin.at[s, xs[d]],
                out_v.at[:, pl.ds(column, SUB)],
                send_sem.at[18],
                fin_sem.at[d, s],
                tensor_0=xs[d],
            ).start()
        out_v[:, pl.ds(column, SUB)] = fin[s, x]

    n_sub = turns * 2 - 1
    arrived(h_buf.at[pl.ds(0, 3), :, 0], send_sem.at[0])
    arrived(w2.at[:, pl.ds(0, 9 * hs)].at[pl.ds(0, half)], send_sem.at[1])
    arrived(fv_stage, send_sem.at[2])
    arrived(h_buf.at[pl.ds(0, n_sub)], send_sem.at[3])
    arrived(w2.at[pl.ds(0, half), pl.ds(0, 9 * hs)], send_sem.at[4])
    arrived(w_relay, send_sem.at[5])
    arrived(fv_plus, send_sem.at[6])
    arrived(fv_minus, send_sem.at[7])
    arrived(a_send, send_sem.at[8])
    arrived(b_send, send_sem.at[9])
    arrived(wo2.at[pl.ds(0, 3 * hs), pl.ds(0, half)], send_sem.at[10])
    arrived(wo2.at[pl.ds(0, 3 * hs), pl.ds(0, half)], send_sem.at[11])
    arrived(wo_relay, send_sem.at[12])
    arrived(att.at[0], send_sem.at[13])
    arrived(att.at[0], send_sem.at[14])
    arrived(att.at[0, near], send_sem.at[15])
    arrived(att.at[0, far], send_sem.at[16])
    for s in range(subs):
        for d in (1, 2, 3):
            column = pl.multiple_of(xs[d] * quarter + s * SUB, 128)
            column = pl.multiple_of(xs[NX - d] * quarter + s * SUB, 128)
            arrived(out_v.at[:, pl.ds(column, SUB)], fin_sem.at[d, s])
    arrived(h_buf.at[pl.ds(0, n_sub)], send_sem.at[17])
    arrived(fin.at[:, pl.ds(0, 3)], send_sem.at[18])
    out[...] = out_v[...]


def body(hidden_in, first_values, qkv_weight, out_weight, mix_table, mix_index, lengths, *, nz):
    rows, model = hidden_in.shape[1:]
    hs = qkv_weight.shape[2]
    quarter = model // NX
    half = quarter // 2
    subs = quarter // SUB
    turns = nz // 2
    block = NX * rows
    vmem = pl.BlockSpec(memory_space=pltpu.VMEM)
    smem = pl.BlockSpec(memory_space=pltpu.SMEM)
    anywhere = pl.BlockSpec(memory_space=pl.ANY)
    dma = pltpu.SemaphoreType.DMA
    scratch = [
        pltpu.VMEM((nz, subs, NX, rows, SUB), BF),
        pltpu.VMEM((quarter, NX * 3 * hs), BF),
        pltpu.VMEM((3, half, hs), BF),
        pltpu.VMEM((NX * hs, quarter), BF),
        pltpu.VMEM((hs, half), BF),
        pltpu.VMEM((NX - 1, nz, rows, hs), BF),
        pltpu.VMEM((nz, NX, rows, hs), BF),
        pltpu.VMEM((turns * (turns + 1) // 2, NX, rows, hs), BF),
        pltpu.VMEM((turns * (turns - 1) // 2, NX, rows, hs), BF),
        pltpu.VMEM((nz, 3, block, 3 * hs), F32),
        pltpu.VMEM((nz, block, 3 * hs), BF),
        pltpu.VMEM((nz, block, 3 * hs), BF),
        pltpu.VMEM((nz, 2, block, 3 * hs), BF),
        pltpu.VMEM((nz, 2, block, 3 * hs), BF),
        pltpu.VMEM((NX, nz, rows, hs), BF),
        pltpu.VMEM((NX, nz, rows, hs), BF),
        pltpu.VMEM((NX, nz, rows, hs), BF),
        pltpu.VMEM((NX, nz, NX, rows, hs), BF),
        pltpu.VMEM((turns, 2, subs, block, SUB), BF),
        pltpu.VMEM((2, turns + 1, subs, block, SUB), BF),
        pltpu.VMEM((subs, NX, rows, SUB), BF),
        pltpu.VMEM((rows, model), BF),
        dma((4,)),
        dma((19,)),
        dma((NX, subs)),
        dma((2, turns, subs)),
        dma((5, 3)),
        dma((7,)),
        dma((NX,)),
        dma((2, turns)),
        dma((2, nz)),
        dma((2, nz)),
        dma((4, NX)),
        dma((2, turns + 1, subs)),
        dma((NX, subs)),
    ]
    result = pl.pallas_call(
        functools.partial(kernel, nz),
        out_shape=jax.ShapeDtypeStruct((rows, model), BF),
        in_specs=[vmem, vmem, anywhere, anywhere, smem, smem, smem],
        out_specs=vmem,
        scratch_shapes=scratch,
        compiler_params=pltpu.CompilerParams(
            collective_id=0, has_side_effects=True, vmem_limit_bytes=60 * 1024 * 1024
        ),
    )(
        hidden_in[0],
        first_values[0],
        jnp.transpose(qkv_weight, (1, 0, 2)),
        out_weight,
        mix_table,
        mix_index,
        lengths,
    )
    return result[None]


def solution(mesh):
    nz = mesh.shape["tensor"] // NX
    torus = Mesh(
        mesh.devices.reshape(mesh.shape["groups"], mesh.shape["dp"], NX, nz),
        ("groups", "dp", "tensor_0", "tensor_1"),
    )
    placed = (
        P(("groups", "dp"), TENSOR, None),
        P(("groups", "dp"), TENSOR, None),
        P(None, None, TENSOR),
        P(TENSOR, None),
        P(),
        P(TENSOR),
        P(("groups", "dp")),
    )
    return jax.shard_map(
        functools.partial(body, nz=nz),
        mesh=torus,
        in_specs=placed,
        out_specs=P(("groups", "dp"), TENSOR, None),
        check_vma=False,
    )
```

time: 490 us -> 156 us (0.32)
  waiting for transfers between devices: 405 us -> 0 us
  Pallas kernels: 0 us -> 152 us
  starting transfers between devices: 29.2 us -> 0 us
  matrix products: 20.8 us -> 0 us
  between operations: 13.9 us -> 1.31 us
  local copies, waits for them, and re-layouts: 10.6 us -> 2.94 us
  other arithmetic: 6.53 us -> 0 us
    reduce_scatter x2 -> x0, waiting for transfers between devices: 267 us -> none  [summed_rows(): subtotal = lax.psum_scatter(subtotal, axis, scatter_dimension=0, tiled=True)]
    pallas_call x0 -> x1, Pallas kernels: none -> 152 us  [body(): pl.pallas_call(functools.partial(kernel, nz), out_shape=jax.ShapeDtypeStr...]
    all_gather x1 -> x0, waiting for transfers between devices: 123 us -> none  [body(): lax.all_gather(local_rows, TENSOR, axis=0, tiled=True)]
    all_to_all x1 -> x0, starting transfers between devices: 29 us -> none  [body(): lax.all_to_all(first_values[0], TENSOR, split_axis=1, concat_axis=0, tile...]
    dot_general x7 -> x0, matrix products: 20.8 us -> none  [the longest x1 9.34 us: body(): jnp.dot(lax.all_gather(local_rows, TENSOR, axis=0, tiled=True), merged_we...]
    all_to_all x1 -> x0, waiting for transfers between devices: 14.2 us -> none  [body(): lax.all_to_all(first_values[0], TENSOR, split_axis=1, concat_axis=0, tile...]
    unnamed x9 -> x2, local copies, waits for them, and re-layouts: 7.86 us -> 2.94 us
  transfers between devices with their start and end apart: 4 -> 0, of which waited for: 4 -> 0; matrix products, arithmetic and copies ran while one was open for 2% -> 0% of each run, Pallas kernels for 0% -> 0%
where the time goes in v1:
time: 156 us
  Pallas kernels  152 us (97%)
  local copies, waits for them, and re-layouts  2.94 us (2%)
    pallas_call x1, Pallas kernels, body(): pl.pallas_call(functools.partial(kernel, nz), out_shape=jax.ShapeDtypeStr...  152 us

profile of v1, /device:TPU:40, one launch (start us, length us, event | category | flops | bytes accessed | tf_op | source)
XLA Modules:
  0.0 155.9 jit_solution(16411883012886637716)
XLA Ops:
  1.3 1.3 copy.8.mix_table
  2.6 151.7 %shard_map.73 = bf16[16,5120]{1,0:T(8,128)(2,1)} custom-call(bf16[16,5120]{1,0:T(8,128)(2,1)} %bitcast.7, bf16[16,8192]{1,0:T(8,128)(2,1)} %bitcast.6, bf16[3,5120,128]{2,1,0:T(8,128)(2,1)} %bitcast.4, bf16[128,5120]{1,0:T(8,128)(2,1)} %w_out.1, f32[8,2]{1,0:T(8,128)} %copy.8.mix_table, s32[1]{0:T(128)S(6)} %copy.10.mix_index, s32[1]{0:T(128)S(6)} %copy.11.lengths), custom_call_target="tpu_custom_call" | custom-call | tf_op jit(solution)/shard_map/pallas_call | solution.py:688
  154.3 1.6 %copy.12 = bf16[1,16,5120]{2,1,0:T(8,128)(2,1)} copy(bf16[1,16,5120]{2,1,0:T(8,128)(2,1)} %bitcast.5) | data formatting | bytes 327680

commit v2 on v1

v2 whole, which is shorter than its diff:
```python
import functools
import math

import jax
import jax.numpy as jnp
from jax import lax
from jax.experimental import pallas as pl
from jax.experimental.pallas import tpu as pltpu
from jax.sharding import Mesh
from jax.sharding import PartitionSpec as P

TENSOR = ("tensor_0", "tensor_1")
NEG_FILL = -1e30
BF = jnp.bfloat16
F32 = jnp.float32
NX = 4
SUB = 256
LAG = 3


def kernel(
    nz,
    hid,
    firsts,
    w_qkv,
    w_out,
    mix_table,
    mix_index,
    lengths,
    out,
    x_wide,
    z_part,
    w2,
    wo2,
    wo_relay,
    fv_stage,
    fv_own,
    fv_plus,
    fv_minus,
    stash,
    b_send,
    b_recv,
    q_buf,
    k_buf,
    v_buf,
    att,
    rs_send,
    rs_recv,
    fin,
    out_v,
    local_sem,
    send_sem,
    own_sem,
    hid_sem,
    ag_sem,
    oz_sem,
    w_sem,
    wo_sem,
    fx_sem,
    fz_sem,
    b_sem,
    att_sem,
    rs_sem,
    fin_sem,
):
    rows, model = hid.shape
    hs = w_qkv.shape[2]
    quarter = model // NX
    half = quarter // 2
    halves = model // 2
    subs = quarter // SUB
    turns = nz // 2
    block = NX * rows

    x = lax.axis_index("tensor_0")
    z = lax.axis_index("tensor_1")
    core = lax.axis_index("dp")
    xs = [x] + [lax.rem(x + d, NX) for d in range(1, NX)]
    z_up = lax.rem(z + 1, nz)
    z_down = lax.rem(z + nz - 1, nz)
    x_way = lax.rem(x + 1 + 2 * core, NX)
    odd = lax.rem(x, 2)
    pair = x + 1 - 2 * odd
    other = lax.rem(x + NX - 1 + 2 * odd, NX)

    def remote(src, dst, send, recv, **where):
        return pltpu.make_async_remote_copy(
            src_ref=src,
            dst_ref=dst,
            send_sem=send,
            recv_sem=recv,
            device_id=where,
            device_id_type=pl.DeviceIdType.MESH,
        )

    def arrived(ref, sem):
        pltpu.make_async_copy(ref, ref, sem).wait()

    barrier = pltpu.get_barrier_semaphore()
    partners = [
        {"dp": 1 - core},
        {"tensor_0": xs[1]},
        {"tensor_0": xs[2]},
        {"tensor_0": xs[3]},
        {"tensor_1": z_up},
        {"tensor_1": z_down},
    ]
    for partner in partners:
        pl.semaphore_signal(
            barrier, inc=1, device_id=partner, device_id_type=pl.DeviceIdType.MESH
        )
    pl.semaphore_wait(barrier, len(partners))

    def half_of(at):
        return lax.rem((at + 1) // 2, 2)

    mine, theirs = half_of(x), 1 - half_of(x)
    stripes, other_stripes = pl.ds(x - odd, 2), pl.ds(NX - 2 - x + odd, 2)
    x_subs, z_subs, z_wide = x_wide.shape[1], z_part.shape[1], z_part.shape[4]

    def x_columns(to_half, s):
        return pl.ds(pl.multiple_of(to_half * halves + s * SUB, 128), SUB)

    def z_columns(to_half, s):
        return pl.ds(pl.multiple_of(to_half * halves + x_subs * SUB + s * z_wide, 128), z_wide)

    def hidden_out(d, to, to_half):
        for s in range(x_subs):
            remote(
                hid.at[:, x_columns(to_half, s)],
                x_wide.at[0, s, x],
                send_sem.at[0],
                hid_sem.at[d, s],
                tensor_0=to,
            ).start()

    for s in range(z_subs):
        remote(
            hid.at[:, z_columns(theirs, s)],
            z_part.at[0, s, x],
            send_sem.at[1],
            hid_sem.at[0, s],
            tensor_0=pair,
        ).start()
    hidden_out(1, pair, theirs)
    hidden_out(2, other, mine)
    hidden_out(3, xs[2], theirs)
    own_hidden = []
    for s in range(z_subs):
        own_hidden.append(
            pltpu.make_async_copy(
                hid.at[:, z_columns(mine, s)], z_part.at[0, s, x], own_sem.at[s]
            )
        )
    for s in range(x_subs):
        own_hidden.append(
            pltpu.make_async_copy(
                hid.at[:, x_columns(mine, s)], x_wide.at[0, s, x], own_sem.at[z_subs + s]
            )
        )
    for copy in own_hidden:
        copy.start()

    def stage_firsts(head, carry):
        away = lax.rem(head - z + nz, nz)
        for d in range(NX):
            column = pl.multiple_of((xs[d] * nz + head) * hs, 128)
            piece = firsts[:, pl.ds(column, hs)]
            if d == 0:
                fv_own[away, x] = piece
            else:
                fv_stage[d - 1, away] = piece
        return carry

    lax.fori_loop(0, nz, stage_firsts, 0)
    for d in (1, 2, 3):
        remote(
            fv_stage.at[d - 1],
            fv_own.at[:, x],
            send_sem.at[2],
            fx_sem.at[d],
            tensor_0=xs[d],
        ).start()

    share = halves // 2
    my_share = pl.multiple_of(core * share, 128)
    sibling_share = pl.multiple_of((1 - core) * share, 128)
    for p in range(3):
        remote(
            w_qkv.at[p, pl.ds(pl.multiple_of(theirs * halves + core * share, 128), share)],
            w2.at[pl.ds(my_share, share), pl.ds((3 + p) * hs, hs)],
            send_sem.at[4],
            w_sem.at[0, p],
            tensor_0=pair,
        ).start()
    own_weights = []
    for p in range(3):
        own_weights.append(
            pltpu.make_async_copy(
                w_qkv.at[p, pl.ds(pl.multiple_of(mine * halves, 128), halves)],
                w2.at[:, pl.ds(p * hs, hs)],
                local_sem.at[p],
            )
        )
    own_weights.append(
        pltpu.make_async_copy(
            w_out.at[:, pl.ds(pl.multiple_of(x * quarter, 128), quarter)],
            wo2.at[pl.ds(0, hs)],
            local_sem.at[3],
        )
    )
    for copy in own_weights:
        copy.start()

    flows = [(0, s) for s in range(x_subs)] + [(1, s) for s in range(z_subs)]

    def longer(way, n):
        return turns if (n % 2 == 0) == (way == 0) else turns - 1

    def part(n, place):
        kind, s = flows[n]
        return x_wide.at[place, s] if kind == 0 else z_part.at[place, s, stripes]

    def ring_send(n, way, step):
        source, target = (step - 1, step) if way else ((nz - step + 1) % nz, nz - step)
        remote(
            part(n, source),
            part(n, target),
            send_sem.at[3 if flows[n][0] == 0 else 5],
            ag_sem.at[way, step - 1, n],
            tensor_1=z_down if way else z_up,
        ).start()

    def to_other(n, place):
        kind, s = flows[n]
        if kind == 1:
            remote(
                z_part.at[place, s, stripes],
                z_part.at[place, s, stripes],
                send_sem.at[6],
                oz_sem.at[place, s],
                tensor_0=other,
            ).start()

    def gather_step(step):
        for n in range(len(flows)):
            for way in (0, 1):
                if step <= longer(way, n):
                    place = step if way else nz - step
                    arrived(part(n, place), ag_sem.at[way, step - 1, n])
                    if step + 1 <= longer(way, n):
                        ring_send(n, way, step + 1)
                    to_other(n, place)

    def weights_step(p):
        here = w2.at[pl.ds(my_share, share), pl.ds((3 + p) * hs, hs)]
        arrived(here, w_sem.at[0, p])
        remote(here, here, send_sem.at[7], w_sem.at[1, p], dp=1 - core).start()

    def weights_last():
        for p in range(3):
            arrived(
                w2.at[pl.ds(sibling_share, share), pl.ds((3 + p) * hs, hs)], w_sem.at[1, p]
            )
        for copy in own_weights:
            copy.wait()

    minus_turns = turns - 1

    def plus_at(step):
        return sum(turns + 1 - u for u in range(1, step))

    def minus_at(step):
        return sum(minus_turns + 1 - u for u in range(1, step))

    def firsts_step(step):
        if step == 0:
            for d in (1, 2, 3):
                arrived(fv_stage.at[d - 1], fx_sem.at[d])
            plus_src = fv_own.at[pl.ds(1, turns)]
            minus_src = fv_own.at[pl.ds(nz - minus_turns, minus_turns)]
        else:
            n_plus = turns + 1 - step
            arrived(fv_plus.at[pl.ds(plus_at(step), n_plus)], fz_sem.at[0, step - 1])
            plus_src = fv_plus.at[pl.ds(plus_at(step) + 1, n_plus - 1)] if n_plus > 1 else None
            n_minus = minus_turns + 1 - step
            minus_src = None
            if n_minus >= 1:
                arrived(fv_minus.at[pl.ds(minus_at(step), n_minus)], fz_sem.at[1, step - 1])
                if n_minus > 1:
                    minus_src = fv_minus.at[pl.ds(minus_at(step), n_minus - 1)]
        if plus_src is not None:
            remote(
                plus_src,
                fv_plus.at[pl.ds(plus_at(step + 1), turns - step)],
                send_sem.at[8],
                fz_sem.at[0, step],
                tensor_1=z_up,
            ).start()
        if minus_src is not None:
            remote(
                minus_src,
                fv_minus.at[pl.ds(minus_at(step + 1), minus_turns - step)],
                send_sem.at[9],
                fz_sem.at[1, step],
                tensor_1=z_down,
            ).start()

    for copy in own_hidden:
        copy.wait()
    for s in range(z_subs):
        arrived(z_part.at[0, s, pair], hid_sem.at[0, s])
        ring_send(x_subs + s, 0, 1)
        ring_send(x_subs + s, 1, 1)
        to_other(x_subs + s, 0)
    for s in range(x_subs):
        for d in (1, 2, 3):
            arrived(x_wide.at[0, s, x], hid_sem.at[d, s])
        ring_send(s, 0, 1)
        ring_send(s, 1, 1)
    early = max(turns - 3, 0)
    weights_after = {2: (0,), 3: (1,)}
    for step in range(1, early + 1):
        gather_step(step)
        firsts_step(step - 1)
        for p in weights_after.get(step, ()):
            weights_step(p)
    for p in range(3):
        if not any(p in done for step, done in weights_after.items() if step <= early):
            weights_step(p)
    weights_last()

    width = 3 * hs

    def place_of(i):
        return jnp.where(i % 2 == 1, (i + 1) // 2, lax.rem(nz - i // 2, nz))

    def project(i):
        place = place_of(i)
        for s in range(z_subs):
            arrived(z_part.at[place, s, other_stripes], oz_sem.at[place, s])
        lhs = jnp.concatenate(
            [x_wide[place, s].reshape(block, SUB) for s in range(x_subs)]
            + [z_part[place, s].reshape(block, z_wide) for s in range(z_subs)],
            axis=1,
        )
        term = jnp.dot(lhs, w2[...], preferred_element_type=F32)
        b_send[i] = term[:, width:].astype(BF)
        remote(
            b_send.at[i], b_recv.at[i], send_sem.at[10], b_sem.at[i], tensor_0=pair
        ).start()
        stash[i] = term[:, :width]

    def finish(i):
        arrived(b_recv.at[i], b_sem.at[i])
        total = stash[i] + b_recv[i].astype(F32)
        total = total.astype(BF).reshape(NX, rows, width)
        origin = lax.rem(z + place_of(i), nz)
        q_buf[:, origin] = total[:, :, :hs]
        k_buf[:, origin] = total[:, :, hs : 2 * hs]
        v_buf[:, origin] = total[:, :, 2 * hs :]

    my_half = pl.multiple_of(core * half, 128)

    def wo_columns(to):
        return pl.ds(pl.multiple_of(to * quarter + core * half, 128), half)

    def wo_piece(r):
        return wo2.at[pl.ds(r * hs, hs), pl.ds(my_half, half)]

    def out_weights_send():
        remote(
            w_out.at[:, wo_columns(xs[2])], wo_relay, send_sem.at[11], wo_sem.at[0], tensor_0=x_way
        ).start()
        for d, r, sem in ((1, 3, 1), (3, 1, 2)):
            remote(
                w_out.at[:, wo_columns(xs[d])],
                wo_piece(r),
                send_sem.at[11],
                wo_sem.at[sem],
                tensor_0=xs[d],
            ).start()

    def out_to_sibling(r):
        remote(
            wo_piece(r), wo_piece(r), send_sem.at[12], wo_sem.at[3 + r], dp=1 - core
        ).start()

    def out_weights_relay():
        arrived(wo_relay, wo_sem.at[0])
        remote(wo_relay, wo_piece(2), send_sem.at[13], wo_sem.at[3], tensor_0=x_way).start()

    def out_weights_direct():
        for r, sem in ((3, 1), (1, 2)):
            arrived(wo_piece(r), wo_sem.at[sem])
            out_to_sibling(r)

    def out_weights_last():
        arrived(wo_piece(2), wo_sem.at[3])
        out_to_sibling(2)

    def out_weights_wait():
        other = pl.multiple_of((1 - core) * half, 128)
        for r in (1, 2, 3):
            arrived(wo2.at[pl.ds(r * hs, hs), pl.ds(other, half)], wo_sem.at[3 + r])

    trips = nz + LAG
    late = {}
    for step in range(early + 1, turns + 1):
        at = min(2 * step - 1, 4 * (step - early) + 1)
        late.setdefault(at, []).append(functools.partial(gather_step, step))
    after_loop = []
    for step in range(early, turns + 1):
        at = 3 + 4 * (step - early)
        if at < trips:
            late.setdefault(at, []).append(functools.partial(firsts_step, step))
        else:
            after_loop.append(step)

    def trip(i, carry):
        for at, steps in late.items():

            @pl.when(i == at)
            def _(steps=steps):
                for step in steps:
                    step()

        @pl.when(i < nz)
        def _():
            project(i)

        @pl.when(i == nz)
        def _():
            out_weights_send()

        @pl.when(i >= LAG)
        def _():
            finish(i - LAG)

        return carry

    lax.fori_loop(0, trips, trip, 0)
    for step in after_loop:
        firsts_step(step)

    row = mix_index[0]
    weight_now = mix_table[0, row]
    weight_first = mix_table[1, row]

    def mix(origin, first):
        now = v_buf[:, origin].astype(F32)
        v_buf[:, origin] = (weight_now * now + weight_first * first.astype(F32)).astype(BF)

    mix(z, fv_own[0])
    for step in range(1, turns + 1):
        mix(lax.rem(z + nz - step, nz), fv_plus[plus_at(step)])
    for step in range(1, minus_turns + 1):
        mix(lax.rem(z + step, nz), fv_minus[minus_at(step) + minus_turns - step])

    scale = 1.0 / math.sqrt(hs)
    valid = lengths[0]
    stripe = nz * rows
    q_blocks = min(nz, 128 // rows)
    q_rows = q_blocks * rows

    def attend(b):
        n = (b + 1) * stripe
        keys = k_buf[0 : b + 1].reshape(n, hs)
        values = v_buf[0 : b + 1].reshape(n, hs)

        def one(t, carry):
            at = pl.ds(t * q_blocks, q_blocks)
            query = q_buf[b, at].reshape(q_rows, hs)
            scores = (
                lax.dot_general(query, keys, (((1,), (1,)), ((), ())), preferred_element_type=F32)
                * scale
            )
            col = lax.broadcasted_iota(jnp.int32, (q_rows, n), 1)
            line = b * stripe + t * q_rows + lax.broadcasted_iota(jnp.int32, (q_rows, n), 0)
            scores = jnp.where((col <= line) & (col < valid), scores, NEG_FILL)
            raised = jnp.exp(scores - jnp.max(scores, axis=1, keepdims=True))
            weights = (raised * (1.0 / jnp.sum(raised, axis=1, keepdims=True))).astype(BF)
            result = jnp.dot(weights, values, preferred_element_type=F32).astype(BF)
            att[0, at, b] = result.reshape(q_blocks, rows, hs)
            return carry

        lax.fori_loop(0, nz // q_blocks, one, 0)

    near, far = pl.ds(0, nz // 2), pl.ds(nz // 2, nz // 2)

    def att_send(b):
        remote(
            att.at[0, :, b], att.at[3, :, b], send_sem.at[14], att_sem.at[0, b], tensor_0=xs[1]
        ).start()
        remote(
            att.at[0, :, b], att.at[1, :, b], send_sem.at[15], att_sem.at[1, b], tensor_0=xs[3]
        ).start()

    def att_pass(b):
        arrived(att.at[3, :, b], att_sem.at[0, b])
        remote(
            att.at[3, near, b], att.at[2, near, b], send_sem.at[16], att_sem.at[2, b], tensor_0=xs[1]
        ).start()
        arrived(att.at[1, :, b], att_sem.at[1, b])
        remote(
            att.at[1, far, b], att.at[2, far, b], send_sem.at[17], att_sem.at[3, b], tensor_0=xs[3]
        ).start()

    attend(0)
    att_send(0)
    out_weights_relay()
    attend(1)
    att_send(1)
    att_pass(0)
    attend(2)
    att_send(2)
    att_pass(1)
    out_weights_direct()
    attend(3)
    att_send(3)
    att_pass(2)
    out_weights_last()
    rs_recv[:, 0] = jnp.zeros(rs_recv.shape[:1] + rs_recv.shape[2:], BF)
    att_pass(3)
    out_weights_wait()
    for b in range(NX):
        arrived(att.at[2, near, b], att_sem.at[2, b])
        arrived(att.at[2, far, b], att_sem.at[3, b])

    def length_of(way, s):
        return turns if (s % 2 == 0) == (way == 0) else turns - 1

    def heads_of(away):
        origin = lax.rem(z + away + nz, nz)
        return jnp.concatenate([att[r, origin].reshape(block, hs) for r in range(NX)], axis=1)

    def columns(s):
        return wo2[:, s * SUB : (s + 1) * SUB]

    def reduce_step(step, carry):
        for s in range(subs):
            for way in (0, 1):
                length = length_of(way, s)
                sign = 1 - 2 * way

                @pl.when(step <= length)
                def _(s=s, way=way, length=length, sign=sign):
                    lhs = heads_of(sign * (length - step + 1))
                    term = jnp.dot(lhs, columns(s), preferred_element_type=F32)

                    @pl.when(step > 1)
                    def _():
                        arrived(rs_recv.at[way, step - 1, s], rs_sem.at[way, step - 1, s])

                    term = term + rs_recv[way, step - 1, s].astype(F32)
                    rs_send[2 * step - 2 + way, s] = term.astype(BF)
                    remote(
                        rs_send.at[2 * step - 2 + way, s],
                        rs_recv.at[way, step, s],
                        send_sem.at[18],
                        rs_sem.at[way, step, s],
                        tensor_1=z_up if way == 0 else z_down,
                    ).start()

        return carry

    lax.fori_loop(1, turns + 1, reduce_step, 0)
    own = heads_of(0)
    for s in range(subs):
        term = jnp.dot(own, columns(s), preferred_element_type=F32)
        for way in (0, 1):
            length = length_of(way, s)
            arrived(rs_recv.at[way, length, s], rs_sem.at[way, length, s])
            term = term + rs_recv[way, length, s].astype(F32)
        fin[s] = term.astype(BF).reshape(NX, rows, SUB)
        column = pl.multiple_of(x * quarter + s * SUB, 128)
        for d in (1, 2, 3):
            remote(
                fin.at[s, xs[d]],
                out_v.at[:, pl.ds(column, SUB)],
                send_sem.at[19],
                fin_sem.at[d, s],
                tensor_0=xs[d],
            ).start()
        out_v[:, pl.ds(column, SUB)] = fin[s, x]

    n_ring = turns * 2 - 1
    arrived(x_wide.at[pl.ds(0, 3), :, 0], send_sem.at[0])
    arrived(z_part.at[0, :, 0], send_sem.at[1])
    arrived(fv_stage, send_sem.at[2])
    arrived(x_wide.at[pl.ds(0, n_ring)], send_sem.at[3])
    arrived(w2.at[pl.ds(0, share), pl.ds(0, width)], send_sem.at[4])
    arrived(z_part.at[pl.ds(0, n_ring), :, pl.ds(0, 2)], send_sem.at[5])
    arrived(z_part.at[:, :, pl.ds(0, 2)], send_sem.at[6])
    arrived(w2.at[pl.ds(0, share), pl.ds(0, width)], send_sem.at[7])
    arrived(fv_plus, send_sem.at[8])
    arrived(fv_minus, send_sem.at[9])
    arrived(b_send, send_sem.at[10])
    arrived(wo2.at[pl.ds(0, 3 * hs), pl.ds(0, half)], send_sem.at[11])
    arrived(wo2.at[pl.ds(0, 3 * hs), pl.ds(0, half)], send_sem.at[12])
    arrived(wo_relay, send_sem.at[13])
    arrived(att.at[0], send_sem.at[14])
    arrived(att.at[0], send_sem.at[15])
    arrived(att.at[0, near], send_sem.at[16])
    arrived(att.at[0, far], send_sem.at[17])
    for s in range(subs):
        for d in (1, 2, 3):
            column = pl.multiple_of(xs[NX - d] * quarter + s * SUB, 128)
            arrived(out_v.at[:, pl.ds(column, SUB)], fin_sem.at[d, s])
    arrived(rs_send.at[pl.ds(0, n_ring)], send_sem.at[18])
    arrived(fin.at[:, pl.ds(0, 3)], send_sem.at[19])
    out[...] = out_v[...]


def body(hidden_in, first_values, qkv_weight, out_weight, mix_table, mix_index, lengths, *, nz):
    rows, model = hidden_in.shape[1:]
    hs = qkv_weight.shape[2]
    quarter = model // NX
    half = quarter // 2
    halves = model // 2
    subs = quarter // SUB
    x_subs = max(1, halves * 3 // 10 // SUB)
    z_subs = 2
    z_wide = (halves - x_subs * SUB) // z_subs
    turns = nz // 2
    block = NX * rows
    vmem = pl.BlockSpec(memory_space=pltpu.VMEM)
    smem = pl.BlockSpec(memory_space=pltpu.SMEM)
    anywhere = pl.BlockSpec(memory_space=pl.ANY)
    dma = pltpu.SemaphoreType.DMA
    scratch = [
        pltpu.VMEM((nz, x_subs, NX, rows, SUB), BF),
        pltpu.VMEM((nz, z_subs, NX, rows, z_wide), BF),
        pltpu.VMEM((halves, 2 * 3 * hs), BF),
        pltpu.VMEM((NX * hs, quarter), BF),
        pltpu.VMEM((hs, half), BF),
        pltpu.VMEM((NX - 1, nz, rows, hs), BF),
        pltpu.VMEM((nz, NX, rows, hs), BF),
        pltpu.VMEM((turns * (turns + 1) // 2, NX, rows, hs), BF),
        pltpu.VMEM((turns * (turns - 1) // 2, NX, rows, hs), BF),
        pltpu.VMEM((nz, block, 3 * hs), F32),
        pltpu.VMEM((nz, block, 3 * hs), BF),
        pltpu.VMEM((nz, block, 3 * hs), BF),
        pltpu.VMEM((NX, nz, rows, hs), BF),
        pltpu.VMEM((NX, nz, rows, hs), BF),
        pltpu.VMEM((NX, nz, rows, hs), BF),
        pltpu.VMEM((NX, nz, NX, rows, hs), BF),
        pltpu.VMEM((2 * turns, subs, block, SUB), BF),
        pltpu.VMEM((2, turns + 1, subs, block, SUB), BF),
        pltpu.VMEM((subs, NX, rows, SUB), BF),
        pltpu.VMEM((rows, model), BF),
        dma((4,)),
        dma((20,)),
        dma((x_subs + z_subs,)),
        dma((NX, x_subs + z_subs)),
        dma((2, turns, x_subs + z_subs)),
        dma((nz, z_subs)),
        dma((2, 3)),
        dma((7,)),
        dma((NX,)),
        dma((2, turns)),
        dma((nz,)),
        dma((4, NX)),
        dma((2, turns + 1, subs)),
        dma((NX, subs)),
    ]
    result = pl.pallas_call(
        functools.partial(kernel, nz),
        out_shape=jax.ShapeDtypeStruct((rows, model), BF),
        in_specs=[vmem, vmem, anywhere, anywhere, smem, smem, smem],
        out_specs=vmem,
        scratch_shapes=scratch,
        compiler_params=pltpu.CompilerParams(
            collective_id=0, has_side_effects=True, vmem_limit_bytes=60 * 1024 * 1024
        ),
    )(
        hidden_in[0],
        first_values[0],
        jnp.transpose(qkv_weight, (1, 0, 2)),
        out_weight,
        mix_table.T,
        mix_index,
        lengths,
    )
    return result[None]


def solution(mesh):
    nz = mesh.shape["tensor"] // NX
    torus = Mesh(
        mesh.devices.reshape(mesh.shape["groups"], mesh.shape["dp"], NX, nz),
        ("groups", "dp", "tensor_0", "tensor_1"),
    )
    placed = (
        P(("groups", "dp"), TENSOR, None),
        P(("groups", "dp"), TENSOR, None),
        P(None, None, TENSOR),
        P(TENSOR, None),
        P(),
        P(TENSOR),
        P(("groups", "dp")),
    )
    return jax.shard_map(
        functools.partial(body, nz=nz),
        mesh=torus,
        in_specs=placed,
        out_specs=P(("groups", "dp"), TENSOR, None),
        check_vma=False,
    )
```

time: 156 us -> 152 us (0.974)
  Pallas kernels: 152 us -> 149 us
    pallas_call x1, Pallas kernels: 152 us -> 149 us  [body(): pl.pallas_call(functools.partial(kernel, nz), out_shape=jax.ShapeDtypeStr...]
where the time goes in v2:
time: 152 us
  Pallas kernels  149 us (98%)
  local copies, waits for them, and re-layouts  1.59 us (1%)
    pallas_call x1, Pallas kernels, body(): pl.pallas_call(functools.partial(kernel, nz), out_shape=jax.ShapeDtypeStr...  149 us

profile of v2, /device:TPU:40, one launch (start us, length us, event | category | flops | bytes accessed | tf_op | source)
XLA Modules:
  0.0 152.3 jit_solution(1255618272550397357)
XLA Ops:
  1.3 149.4 %shard_map.73 = bf16[16,5120]{1,0:T(8,128)(2,1)} custom-call(bf16[16,5120]{1,0:T(8,128)(2,1)} %bitcast.8, bf16[16,8192]{1,0:T(8,128)(2,1)} %bitcast.7, bf16[3,5120,128]{2,1,0:T(8,128)(2,1)} %bitcast.5, bf16[128,5120]{1,0:T(8,128)(2,1)} %w_out.1, f32[2,8]{1,0:T(2,128)} %bitcast.9, s32[1]{0:T(128)S(6)} %copy.9.mix_index, s32[1]{0:T(128)S(6)} %copy.10.lengths), custom_call_target="tpu_custom_call" | custom-call | tf_op jit(solution)/shard_map/pallas_call | solution.py:667
  150.7 1.6 %copy.11 = bf16[1,16,5120]{2,1,0:T(8,128)(2,1)} copy(bf16[1,16,5120]{2,1,0:T(8,128)(2,1)} %bitcast.6) | data formatting | bytes 327680

commit v3 on v2

--- a/solution.py
+++ b/solution.py
@@ -35,8 +35,7 @@
     wo_relay,
     fv_stage,
     fv_own,
-    fv_plus,
-    fv_minus,
+    fv_in,
     stash,
     b_send,
     b_recv,
@@ -47,7 +46,6 @@
     rs_send,
     rs_recv,
     fin,
-    out_v,
     local_sem,
     send_sem,
     own_sem,
@@ -212,6 +210,52 @@
     for copy in own_weights:
         copy.start()
 
+    my_half = pl.multiple_of(core * half, 128)
+
+    def wo_columns(to):
+        return pl.ds(pl.multiple_of(to * quarter + core * half, 128), half)
+
+    def wo_piece(r):
+        return wo2.at[pl.ds(r * hs, hs), pl.ds(my_half, half)]
+
+    def out_weights_send():
+        remote(
+            w_out.at[:, wo_columns(xs[2])], wo_relay, send_sem.at[11], wo_sem.at[0], tensor_0=x_way
+        ).start()
+        for d, r, sem in ((1, 3, 1), (3, 1, 2)):
+            remote(
+                w_out.at[:, wo_columns(xs[d])],
+                wo_piece(r),
+                send_sem.at[11],
+                wo_sem.at[sem],
+                tensor_0=xs[d],
+            ).start()
+
+    def out_to_sibling(r):
+        remote(
+            wo_piece(r), wo_piece(r), send_sem.at[12], wo_sem.at[3 + r], dp=1 - core
+        ).start()
+
+    def out_weights_relay():
+        arrived(wo_relay, wo_sem.at[0])
+        remote(wo_relay, wo_piece(2), send_sem.at[13], wo_sem.at[3], tensor_0=x_way).start()
+
+    def out_weights_direct():
+        for r, sem in ((3, 1), (1, 2)):
+            arrived(wo_piece(r), wo_sem.at[sem])
+            out_to_sibling(r)
+
+    def out_weights_last():
+        arrived(wo_piece(2), wo_sem.at[3])
+        out_to_sibling(2)
+
+    def out_weights_wait():
+        other = pl.multiple_of((1 - core) * half, 128)
+        for r in (1, 2, 3):
+            arrived(wo2.at[pl.ds(r * hs, hs), pl.ds(other, half)], wo_sem.at[3 + r])
+
+    out_weights_send()
+
     flows = [(0, s) for s in range(x_subs)] + [(1, s) for s in range(z_subs)]
 
     def longer(way, n):
@@ -265,45 +309,17 @@
         for copy in own_weights:
             copy.wait()
 
-    minus_turns = turns - 1
-
-    def plus_at(step):
-        return sum(turns + 1 - u for u in range(1, step))
-
-    def minus_at(step):
-        return sum(minus_turns + 1 - u for u in range(1, step))
-
     def firsts_step(step):
-        if step == 0:
+        if step == 1:
             for d in (1, 2, 3):
                 arrived(fv_stage.at[d - 1], fx_sem.at[d])
-            plus_src = fv_own.at[pl.ds(1, turns)]
-            minus_src = fv_own.at[pl.ds(nz - minus_turns, minus_turns)]
-        else:
-            n_plus = turns + 1 - step
-            arrived(fv_plus.at[pl.ds(plus_at(step), n_plus)], fz_sem.at[0, step - 1])
-            plus_src = fv_plus.at[pl.ds(plus_at(step) + 1, n_plus - 1)] if n_plus > 1 else None
-            n_minus = minus_turns + 1 - step
-            minus_src = None
-            if n_minus >= 1:
-                arrived(fv_minus.at[pl.ds(minus_at(step), n_minus)], fz_sem.at[1, step - 1])
-                if n_minus > 1:
-                    minus_src = fv_minus.at[pl.ds(minus_at(step), n_minus - 1)]
-        if plus_src is not None:
+        for away in sorted({step, nz - step}):
             remote(
-                plus_src,
-                fv_plus.at[pl.ds(plus_at(step + 1), turns - step)],
+                fv_own.at[away],
+                fv_in.at[nz - away],
                 send_sem.at[8],
-                fz_sem.at[0, step],
-                tensor_1=z_up,
-            ).start()
-        if minus_src is not None:
-            remote(
-                minus_src,
-                fv_minus.at[pl.ds(minus_at(step + 1), minus_turns - step)],
-                send_sem.at[9],
-                fz_sem.at[1, step],
-                tensor_1=z_down,
+                fz_sem.at[nz - away],
+                tensor_1=lax.rem(z + away, nz),
             ).start()
 
     for copy in own_hidden:
@@ -318,11 +334,11 @@
             arrived(x_wide.at[0, s, x], hid_sem.at[d, s])
         ring_send(s, 0, 1)
         ring_send(s, 1, 1)
-    early = max(turns - 3, 0)
+    early = max(turns - 4, 0)
     weights_after = {2: (0,), 3: (1,)}
     for step in range(1, early + 1):
         gather_step(step)
-        firsts_step(step - 1)
+        firsts_step(step)
         for p in weights_after.get(step, ()):
             weights_step(p)
     for p in range(3):
@@ -360,62 +376,21 @@
         k_buf[:, origin] = total[:, :, hs : 2 * hs]
         v_buf[:, origin] = total[:, :, 2 * hs :]
 
-    my_half = pl.multiple_of(core * half, 128)
-
-    def wo_columns(to):
-        return pl.ds(pl.multiple_of(to * quarter + core * half, 128), half)
-
-    def wo_piece(r):
-        return wo2.at[pl.ds(r * hs, hs), pl.ds(my_half, half)]
-
-    def out_weights_send():
-        remote(
-            w_out.at[:, wo_columns(xs[2])], wo_relay, send_sem.at[11], wo_sem.at[0], tensor_0=x_way
-        ).start()
-        for d, r, sem in ((1, 3, 1), (3, 1, 2)):
-            remote(
-                w_out.at[:, wo_columns(xs[d])],
-                wo_piece(r),
-                send_sem.at[11],
-                wo_sem.at[sem],
-                tensor_0=xs[d],
-            ).start()
-
-    def out_to_sibling(r):
-        remote(
-            wo_piece(r), wo_piece(r), send_sem.at[12], wo_sem.at[3 + r], dp=1 - core
-        ).start()
-
-    def out_weights_relay():
-        arrived(wo_relay, wo_sem.at[0])
-        remote(wo_relay, wo_piece(2), send_sem.at[13], wo_sem.at[3], tensor_0=x_way).start()
-
-    def out_weights_direct():
-        for r, sem in ((3, 1), (1, 2)):
-            arrived(wo_piece(r), wo_sem.at[sem])
-            out_to_sibling(r)
-
-    def out_weights_last():
-        arrived(wo_piece(2), wo_sem.at[3])
-        out_to_sibling(2)
-
-    def out_weights_wait():
-        other = pl.multiple_of((1 - core) * half, 128)
-        for r in (1, 2, 3):
-            arrived(wo2.at[pl.ds(r * hs, hs), pl.ds(other, half)], wo_sem.at[3 + r])
-
     trips = nz + LAG
     late = {}
-    for step in range(early + 1, turns + 1):
-        at = min(2 * step - 1, 4 * (step - early) + 1)
-        late.setdefault(at, []).append(functools.partial(gather_step, step))
-    after_loop = []
-    for step in range(early, turns + 1):
-        at = 3 + 4 * (step - early)
-        if at < trips:
-            late.setdefault(at, []).append(functools.partial(firsts_step, step))
-        else:
-            after_loop.append(step)
+
+    def at_trip(i, *steps):
+        late.setdefault(min(i, trips - 1), []).extend(steps)
+
+    for step, at in zip(range(early + 1, turns + 1), (0, 3, 8, 13)):
+        at_trip(
+            min(at, 2 * step - 1),
+            functools.partial(gather_step, step),
+            functools.partial(firsts_step, step),
+        )
+    at_trip(4, out_weights_relay)
+    at_trip(6, out_weights_direct)
+    at_trip(12, out_weights_last)
 
     def trip(i, carry):
         for at, steps in late.items():
@@ -429,10 +404,6 @@
         def _():
             project(i)
 
-        @pl.when(i == nz)
-        def _():
-            out_weights_send()
-
         @pl.when(i >= LAG)
         def _():
             finish(i - LAG)
@@ -440,8 +411,7 @@
         return carry
 
     lax.fori_loop(0, trips, trip, 0)
-    for step in after_loop:
-        firsts_step(step)
+    out_weights_wait()
 
     row = mix_index[0]
     weight_now = mix_table[0, row]
@@ -452,10 +422,9 @@
         v_buf[:, origin] = (weight_now * now + weight_first * first.astype(F32)).astype(BF)
 
     mix(z, fv_own[0])
-    for step in range(1, turns + 1):
-        mix(lax.rem(z + nz - step, nz), fv_plus[plus_at(step)])
-    for step in range(1, minus_turns + 1):
-        mix(lax.rem(z + step, nz), fv_minus[minus_at(step) + minus_turns - step])
+    for away in range(1, nz):
+        arrived(fv_in.at[away], fz_sem.at[away])
+        mix(lax.rem(z + away, nz), fv_in[away])
 
     scale = 1.0 / math.sqrt(hs)
     valid = lengths[0]
@@ -508,21 +477,17 @@
 
     attend(0)
     att_send(0)
-    out_weights_relay()
     attend(1)
     att_send(1)
     att_pass(0)
     attend(2)
     att_send(2)
     att_pass(1)
-    out_weights_direct()
     attend(3)
     att_send(3)
     att_pass(2)
-    out_weights_last()
     rs_recv[:, 0] = jnp.zeros(rs_recv.shape[:1] + rs_recv.shape[2:], BF)
     att_pass(3)
-    out_weights_wait()
     for b in range(NX):
         arrived(att.at[2, near, b], att_sem.at[2, b])
         arrived(att.at[2, far, b], att_sem.at[3, b])
@@ -577,12 +542,14 @@
         for d in (1, 2, 3):
             remote(
                 fin.at[s, xs[d]],
-                out_v.at[:, pl.ds(column, SUB)],
+                out.at[:, pl.ds(column, SUB)],
                 send_sem.at[19],
                 fin_sem.at[d, s],
                 tensor_0=xs[d],
             ).start()
-        out_v[:, pl.ds(column, SUB)] = fin[s, x]
+        pltpu.make_async_copy(
+            fin.at[s, x], out.at[:, pl.ds(column, SUB)], fin_sem.at[0, s]
+        ).start()
 
     n_ring = turns * 2 - 1
     arrived(x_wide.at[pl.ds(0, 3), :, 0], send_sem.at[0])
@@ -593,8 +560,7 @@
     arrived(z_part.at[pl.ds(0, n_ring), :, pl.ds(0, 2)], send_sem.at[5])
     arrived(z_part.at[:, :, pl.ds(0, 2)], send_sem.at[6])
     arrived(w2.at[pl.ds(0, share), pl.ds(0, width)], send_sem.at[7])
-    arrived(fv_plus, send_sem.at[8])
-    arrived(fv_minus, send_sem.at[9])
+    arrived(fv_own.at[pl.ds(1, nz - 1)], send_sem.at[8])
     arrived(b_send, send_sem.at[10])
     arrived(wo2.at[pl.ds(0, 3 * hs), pl.ds(0, half)], send_sem.at[11])
     arrived(wo2.at[pl.ds(0, 3 * hs), pl.ds(0, half)], send_sem.at[12])
@@ -604,12 +570,10 @@
     arrived(att.at[0, near], send_sem.at[16])
     arrived(att.at[0, far], send_sem.at[17])
     for s in range(subs):
-        for d in (1, 2, 3):
-            column = pl.multiple_of(xs[NX - d] * quarter + s * SUB, 128)
-            arrived(out_v.at[:, pl.ds(column, SUB)], fin_sem.at[d, s])
+        for d in range(NX):
+            arrived(fin.at[s, x], fin_sem.at[d, s])
     arrived(rs_send.at[pl.ds(0, n_ring)], send_sem.at[18])
     arrived(fin.at[:, pl.ds(0, 3)], send_sem.at[19])
-    out[...] = out_v[...]
 
 
 def body(hidden_in, first_values, qkv_weight, out_weight, mix_table, mix_index, lengths, *, nz):
@@ -636,8 +600,7 @@
         pltpu.VMEM((hs, half), BF),
         pltpu.VMEM((NX - 1, nz, rows, hs), BF),
         pltpu.VMEM((nz, NX, rows, hs), BF),
-        pltpu.VMEM((turns * (turns + 1) // 2, NX, rows, hs), BF),
-        pltpu.VMEM((turns * (turns - 1) // 2, NX, rows, hs), BF),
+        pltpu.VMEM((nz, NX, rows, hs), BF),
         pltpu.VMEM((nz, block, 3 * hs), F32),
         pltpu.VMEM((nz, block, 3 * hs), BF),
         pltpu.VMEM((nz, block, 3 * hs), BF),
@@ -648,7 +611,6 @@
         pltpu.VMEM((2 * turns, subs, block, SUB), BF),
         pltpu.VMEM((2, turns + 1, subs, block, SUB), BF),
         pltpu.VMEM((subs, NX, rows, SUB), BF),
-        pltpu.VMEM((rows, model), BF),
         dma((4,)),
         dma((20,)),
         dma((x_subs + z_subs,)),
@@ -658,7 +620,7 @@
         dma((2, 3)),
         dma((7,)),
         dma((NX,)),
-        dma((2, turns)),
+        dma((nz,)),
         dma((nz,)),
         dma((4, NX)),
         dma((2, turns + 1, subs)),
@@ -668,7 +630,7 @@
         functools.partial(kernel, nz),
         out_shape=jax.ShapeDtypeStruct((rows, model), BF),
         in_specs=[vmem, vmem, anywhere, anywhere, smem, smem, smem],
-        out_specs=vmem,
+        out_specs=anywhere,
         scratch_shapes=scratch,
         compiler_params=pltpu.CompilerParams(
             collective_id=0, has_side_effects=True, vmem_limit_bytes=60 * 1024 * 1024

time: 152 us -> 143 us (0.941)
  Pallas kernels: 149 us -> 140 us
    pallas_call x1, Pallas kernels: 149 us -> 140 us  [body(): pl.pallas_call(functools.partial(kernel, nz), out_shape=jax.ShapeDtypeStr...]
where the time goes in v3:
time: 143 us
  Pallas kernels  140 us (98%)
  local copies, waits for them, and re-layouts  1.59 us (1%)
    pallas_call x1, Pallas kernels, body(): pl.pallas_call(functools.partial(kernel, nz), out_shape=jax.ShapeDtypeStr...  140 us

profile of v3, /device:TPU:40, one launch (start us, length us, event | category | flops | bytes accessed | tf_op | source)
XLA Modules:
  0.0 142.8 jit_solution(17506356054153433300)
XLA Ops:
  1.3 139.9 %shard_map.73 = bf16[16,5120]{1,0:T(8,128)(2,1)} custom-call(bf16[16,5120]{1,0:T(8,128)(2,1)} %bitcast.8, bf16[16,8192]{1,0:T(8,128)(2,1)} %bitcast.7, bf16[3,5120,128]{2,1,0:T(8,128)(2,1)} %bitcast.5, bf16[128,5120]{1,0:T(8,128)(2,1)} %w_out.1, f32[2,8]{1,0:T(2,128)} %bitcast.9, s32[1]{0:T(128)S(6)} %copy.9.mix_index, s32[1]{0:T(128)S(6)} %copy.10.lengths), custom_call_target="tpu_custom_call" | custom-call | tf_op jit(solution)/shard_map/pallas_call | solution.py:629
  141.3 1.6 %copy.11 = bf16[1,16,5120]{2,1,0:T(8,128)(2,1)} copy(bf16[1,16,5120]{2,1,0:T(8,128)(2,1)} %bitcast.6) | data formatting | bytes 327680

commit v4 on v3

--- a/solution.py
+++ b/solution.py
@@ -334,8 +334,8 @@
             arrived(x_wide.at[0, s, x], hid_sem.at[d, s])
         ring_send(s, 0, 1)
         ring_send(s, 1, 1)
-    early = max(turns - 4, 0)
-    weights_after = {2: (0,), 3: (1,)}
+    early = max(turns - 3, 0)
+    weights_after = {2: (0,), 3: (1,), 4: (2,)}
     for step in range(1, early + 1):
         gather_step(step)
         firsts_step(step)
@@ -382,7 +382,7 @@
     def at_trip(i, *steps):
         late.setdefault(min(i, trips - 1), []).extend(steps)
 
-    for step, at in zip(range(early + 1, turns + 1), (0, 3, 8, 13)):
+    for step, at in zip(range(early + 1, turns + 1), (2, 7, 12)):
         at_trip(
             min(at, 2 * step - 1),
             functools.partial(gather_step, step),

time: 143 us -> 145 us (1.014)
  Pallas kernels: 140 us -> 142 us
    pallas_call x1, Pallas kernels: 140 us -> 142 us  [body(): pl.pallas_call(functools.partial(kernel, nz), out_shape=jax.ShapeDtypeStr...]
where the time goes in v4:
time: 145 us
  Pallas kernels  142 us (98%)
  local copies, waits for them, and re-layouts  1.59 us (1%)
    pallas_call x1, Pallas kernels, body(): pl.pallas_call(functools.partial(kernel, nz), out_shape=jax.ShapeDtypeStr...  142 us

profile of v4, /device:TPU:40, one launch (start us, length us, event | category | flops | bytes accessed | tf_op | source)
XLA Modules:
  0.0 144.9 jit_solution(1585344760180881777)
XLA Ops:
  1.3 142.0 %shard_map.73 = bf16[16,5120]{1,0:T(8,128)(2,1)} custom-call(bf16[16,5120]{1,0:T(8,128)(2,1)} %bitcast.8, bf16[16,8192]{1,0:T(8,128)(2,1)} %bitcast.7, bf16[3,5120,128]{2,1,0:T(8,128)(2,1)} %bitcast.5, bf16[128,5120]{1,0:T(8,128)(2,1)} %w_out.1, f32[2,8]{1,0:T(2,128)} %bitcast.9, s32[1]{0:T(128)S(6)} %copy.9.mix_index, s32[1]{0:T(128)S(6)} %copy.10.lengths), custom_call_target="tpu_custom_call" | custom-call | tf_op jit(solution)/shard_map/pallas_call | solution.py:629
  143.3 1.6 %copy.11 = bf16[1,16,5120]{2,1,0:T(8,128)(2,1)} copy(bf16[1,16,5120]{2,1,0:T(8,128)(2,1)} %bitcast.6) | data formatting | bytes 327680

commit v5 on v4

--- a/solution.py
+++ b/solution.py
@@ -45,6 +45,7 @@
     att,
     rs_send,
     rs_recv,
+    own_term,
     fin,
     local_sem,
     send_sem,
@@ -338,7 +339,6 @@
     weights_after = {2: (0,), 3: (1,), 4: (2,)}
     for step in range(1, early + 1):
         gather_step(step)
-        firsts_step(step)
         for p in weights_after.get(step, ()):
             weights_step(p)
     for p in range(3):
@@ -383,11 +383,12 @@
         late.setdefault(min(i, trips - 1), []).extend(steps)
 
     for step, at in zip(range(early + 1, turns + 1), (2, 7, 12)):
-        at_trip(
-            min(at, 2 * step - 1),
-            functools.partial(gather_step, step),
-            functools.partial(firsts_step, step),
-        )
+        at_trip(min(at, 2 * step - 1), functools.partial(gather_step, step))
+        if step == turns:
+            at_trip(
+                min(at, 2 * step - 1),
+                *(functools.partial(firsts_step, away) for away in range(1, turns + 1)),
+            )
     at_trip(4, out_weights_relay)
     at_trip(6, out_weights_direct)
     at_trip(12, out_weights_last)
@@ -475,19 +476,12 @@
             att.at[1, far, b], att.at[2, far, b], send_sem.at[17], att_sem.at[3, b], tensor_0=xs[3]
         ).start()
 
-    attend(0)
-    att_send(0)
-    attend(1)
-    att_send(1)
-    att_pass(0)
-    attend(2)
-    att_send(2)
-    att_pass(1)
-    attend(3)
-    att_send(3)
-    att_pass(2)
+    for b in range(NX):
+        attend(b)
+        att_send(b)
     rs_recv[:, 0] = jnp.zeros(rs_recv.shape[:1] + rs_recv.shape[2:], BF)
-    att_pass(3)
+    for b in range(NX):
+        att_pass(b)
     for b in range(NX):
         arrived(att.at[2, near, b], att_sem.at[2, b])
         arrived(att.at[2, far, b], att_sem.at[3, b])
@@ -501,54 +495,82 @@
 
     def columns(s):
         return wo2[:, s * SUB : (s + 1) * SUB]
+
+    def own_terms(step):
+        for s in range(subs):
+            for way in (0, 1):
+                length = length_of(way, s)
+
+                @pl.when(step <= length)
+                def _(s=s, way=way, length=length):
+                    lhs = heads_of((1 - 2 * way) * (length - step + 1))
+                    own_term[way, s] = jnp.dot(lhs, columns(s), preferred_element_type=F32)
+
+    def out_columns(s):
+        return pl.ds(pl.multiple_of(x * quarter + s * SUB, 128), SUB)
 
     def reduce_step(step, carry):
         for s in range(subs):
             for way in (0, 1):
                 length = length_of(way, s)
-                sign = 1 - 2 * way
+                z_next = z_down if way else z_up
+                slot = 2 * step - 2 + way
 
                 @pl.when(step <= length)
-                def _(s=s, way=way, length=length, sign=sign):
-                    lhs = heads_of(sign * (length - step + 1))
-                    term = jnp.dot(lhs, columns(s), preferred_element_type=F32)
-
+                def _(s=s, way=way, z_next=z_next, slot=slot, length=length):
                     @pl.when(step > 1)
                     def _():
                         arrived(rs_recv.at[way, step - 1, s], rs_sem.at[way, step - 1, s])
 
-                    term = term + rs_recv[way, step - 1, s].astype(F32)
-                    rs_send[2 * step - 2 + way, s] = term.astype(BF)
-                    remote(
-                        rs_send.at[2 * step - 2 + way, s],
-                        rs_recv.at[way, step, s],
-                        send_sem.at[18],
-                        rs_sem.at[way, step, s],
-                        tensor_1=z_up if way == 0 else z_down,
-                    ).start()
+                    term = own_term[way, s] + rs_recv[way, step - 1, s].reshape(
+                        block, SUB
+                    ).astype(F32)
+                    rs_send[slot, s] = term.astype(BF).reshape(NX, rows, SUB)
+
+                    @pl.when(step < length)
+                    def _():
+                        remote(
+                            rs_send.at[slot, s],
+                            rs_recv.at[way, step, s],
+                            send_sem.at[18],
+                            rs_sem.at[way, step, s],
+                            tensor_1=z_next,
+                        ).start()
+
+                    @pl.when(step == length)
+                    def _():
+                        for d in range(NX):
+                            remote(
+                                rs_send.at[slot, s, xs[d]],
+                                out.at[1 + way, :, out_columns(s)],
+                                send_sem.at[18],
+                                fin_sem.at[1 + way, d, s],
+                                tensor_0=xs[d],
+                                tensor_1=z_next,
+                            ).start()
+
+        @pl.when(step < turns)
+        def _():
+            own_terms(step + 1)
 
         return carry
 
+    own_terms(1)
     lax.fori_loop(1, turns + 1, reduce_step, 0)
     own = heads_of(0)
     for s in range(subs):
         term = jnp.dot(own, columns(s), preferred_element_type=F32)
-        for way in (0, 1):
-            length = length_of(way, s)
-            arrived(rs_recv.at[way, length, s], rs_sem.at[way, length, s])
-            term = term + rs_recv[way, length, s].astype(F32)
         fin[s] = term.astype(BF).reshape(NX, rows, SUB)
-        column = pl.multiple_of(x * quarter + s * SUB, 128)
         for d in (1, 2, 3):
             remote(
                 fin.at[s, xs[d]],
-                out.at[:, pl.ds(column, SUB)],
+                out.at[0, :, out_columns(s)],
                 send_sem.at[19],
-                fin_sem.at[d, s],
+                fin_sem.at[0, d, s],
                 tensor_0=xs[d],
             ).start()
         pltpu.make_async_copy(
-            fin.at[s, x], out.at[:, pl.ds(column, SUB)], fin_sem.at[0, s]
+            fin.at[s, x], out.at[0, :, out_columns(s)], fin_sem.at[0, 0, s]
         ).start()
 
     n_ring = turns * 2 - 1
@@ -571,7 +593,8 @@
     arrived(att.at[0, far], send_sem.at[17])
     for s in range(subs):
         for d in range(NX):
-            arrived(fin.at[s, x], fin_sem.at[d, s])
+            for piece in range(3):
+                arrived(fin.at[s, x], fin_sem.at[piece, d, s])
     arrived(rs_send.at[pl.ds(0, n_ring)], send_sem.at[18])
     arrived(fin.at[:, pl.ds(0, 3)], send_sem.at[19])
 
@@ -583,7 +606,7 @@
     half = quarter // 2
     halves = model // 2
     subs = quarter // SUB
-    x_subs = max(1, halves * 3 // 10 // SUB)
+    x_subs = max(1, halves * 4 // 10 // SUB)
     z_subs = 2
     z_wide = (halves - x_subs * SUB) // z_subs
     turns = nz // 2
@@ -608,8 +631,9 @@
         pltpu.VMEM((NX, nz, rows, hs), BF),
         pltpu.VMEM((NX, nz, rows, hs), BF),
         pltpu.VMEM((NX, nz, NX, rows, hs), BF),
-        pltpu.VMEM((2 * turns, subs, block, SUB), BF),
-        pltpu.VMEM((2, turns + 1, subs, block, SUB), BF),
+        pltpu.VMEM((2 * turns, subs, NX, rows, SUB), BF),
+        pltpu.VMEM((2, turns, subs, NX, rows, SUB), BF),
+        pltpu.VMEM((2, subs, block, SUB), F32),
         pltpu.VMEM((subs, NX, rows, SUB), BF),
         dma((4,)),
         dma((20,)),
@@ -623,12 +647,12 @@
         dma((nz,)),
         dma((nz,)),
         dma((4, NX)),
-        dma((2, turns + 1, subs)),
-        dma((NX, subs)),
+        dma((2, turns, subs)),
+        dma((3, NX, subs)),
     ]
     result = pl.pallas_call(
         functools.partial(kernel, nz),
-        out_shape=jax.ShapeDtypeStruct((rows, model), BF),
+        out_shape=jax.ShapeDtypeStruct((3, rows, model), BF),
         in_specs=[vmem, vmem, anywhere, anywhere, smem, smem, smem],
         out_specs=anywhere,
         scratch_shapes=scratch,
@@ -644,7 +668,8 @@
         mix_index,
         lengths,
     )
-    return result[None]
+    first, second, third = (piece.astype(F32) for piece in result)
+    return (first + second + third).astype(BF)[None]
 
 
 def solution(mesh):

time: 145 us -> 137 us (0.945)
  Pallas kernels: 142 us -> 133 us
  other arithmetic: 0 us -> 1.8 us
  local copies, waits for them, and re-layouts: 1.59 us -> 0 us
    pallas_call x1, Pallas kernels: 142 us -> 133 us  [body(): pl.pallas_call(functools.partial(kernel, nz), out_shape=jax.ShapeDtypeStr...]
    convert_element_type x0 -> x1, other arithmetic: none -> 1.8 us  [body(): return (first + second + third).astype(BF)[None]]
    unnamed x1 -> x0, local copies, waits for them, and re-layouts: 1.59 us -> none
where the time goes in v5:
time: 137 us
  Pallas kernels  133 us (97%)
  other arithmetic  1.8 us (1%)
    pallas_call x1, Pallas kernels, body(): pl.pallas_call(functools.partial(kernel, nz), out_shape=jax.ShapeDtypeStr...  133 us

profile of v5, /device:TPU:40, one launch (start us, length us, event | category | flops | bytes accessed | tf_op | source)
XLA Modules:
  0.0 136.6 jit_solution(14458826299984804277)
XLA Ops:
  1.3 133.5 %shard_map.73 = bf16[3,16,5120]{2,1,0:T(8,128)(2,1)} custom-call(bf16[16,5120]{1,0:T(8,128)(2,1)} %bitcast.6, bf16[16,8192]{1,0:T(8,128)(2,1)} %bitcast.5, bf16[3,5120,128]{2,1,0:T(8,128)(2,1)} %bitcast.4, bf16[128,5120]{1,0:T(8,128)(2,1)} %w_out.1, f32[2,8]{1,0:T(2,128)} %bitcast.7, s32[1]{0:T(128)S(6)} %copy.8.mix_index, s32[1]{0:T(128)S(6)} %copy.9.lengths), custom_call_target="tpu_custom_call" | custom-call | tf_op jit(solution)/shard_map/pallas_call | solution.py:653
  134.8 1.8 %add_convert_fusion = bf16[1,16,5120]{2,1,0:T(8,128)(2,1)} fusion(bf16[3,16,5120]{2,1,0:T(8,128)(2,1)} %shard_map.73), kind=kLoop, calls=%fused_computation | loop fusion | flops 491520 | bytes 655360 | tf_op jit(solution)/shard_map/convert_element_type | solution.py:672

commit v6 on v5

--- a/solution.py
+++ b/solution.py
@@ -476,102 +476,92 @@
             att.at[1, far, b], att.at[2, far, b], send_sem.at[17], att_sem.at[3, b], tensor_0=xs[3]
         ).start()
 
+    my_columns = pl.ds(pl.multiple_of(x * quarter, 128), quarter)
+
+    def length_of(way, b):
+        return turns if (b % 2 == 0) == (way == 0) else turns - 1
+
+    def ready(b):
+        arrived(att.at[2, near, b], att_sem.at[2, b])
+        arrived(att.at[2, far, b], att_sem.at[3, b])
+        lhs = jnp.concatenate([att[r, :, b].reshape(stripe, hs) for r in range(NX)], axis=1)
+        for s in range(subs):
+            column = slice(s * SUB, (s + 1) * SUB)
+            term = jnp.dot(lhs, wo2[:, column], preferred_element_type=F32)
+            own_term[b, :, :, column] = term.reshape(nz, rows, SUB)
+        fin[b] = own_term[b, z].astype(BF)
+
+    def reduce_step(b, step):
+        for way in (0, 1):
+            length = length_of(way, b)
+            slot = (2 * b + way) * turns + step
+            z_next = z_down if way else z_up
+
+            def one(b=b, way=way, length=length, slot=slot, z_next=z_next):
+                target = lax.rem(z + (1 - 2 * way) * (length - step + 1) + nz, nz)
+                term = own_term[b, target]
+                if not (isinstance(step, int) and step == 1):
+                    arrived(rs_recv.at[slot - 1], rs_sem.at[slot - 1])
+                    term = term + rs_recv[slot - 1].astype(F32)
+                rs_send[slot - 1] = term.astype(BF)
+
+                def go_on():
+                    remote(
+                        rs_send.at[slot - 1],
+                        rs_recv.at[slot],
+                        send_sem.at[18],
+                        rs_sem.at[slot],
+                        tensor_1=z_next,
+                    ).start()
+
+                def deliver():
+                    remote(
+                        rs_send.at[slot - 1],
+                        out.at[1 + way, :, my_columns],
+                        send_sem.at[18],
+                        fin_sem.at[1 + way, lax.rem(b - x + NX, NX)],
+                        tensor_0=jnp.int32(b),
+                        tensor_1=z_next,
+                    ).start()
+
+                if isinstance(step, int):
+                    (go_on if step < length else deliver)()
+                else:
+                    pl.when(step < length)(go_on)
+                    pl.when(step == length)(deliver)
+
+            if isinstance(step, int):
+                if step <= length:
+                    one()
+            else:
+                pl.when(step <= length)(one)
+
     for b in range(NX):
         attend(b)
         att_send(b)
-    rs_recv[:, 0] = jnp.zeros(rs_recv.shape[:1] + rs_recv.shape[2:], BF)
+    att_pass(0)
     for b in range(NX):
-        att_pass(b)
-    for b in range(NX):
-        arrived(att.at[2, near, b], att_sem.at[2, b])
-        arrived(att.at[2, far, b], att_sem.at[3, b])
-
-    def length_of(way, s):
-        return turns if (s % 2 == 0) == (way == 0) else turns - 1
-
-    def heads_of(away):
-        origin = lax.rem(z + away + nz, nz)
-        return jnp.concatenate([att[r, origin].reshape(block, hs) for r in range(NX)], axis=1)
-
-    def columns(s):
-        return wo2[:, s * SUB : (s + 1) * SUB]
-
-    def own_terms(step):
-        for s in range(subs):
-            for way in (0, 1):
-                length = length_of(way, s)
-
-                @pl.when(step <= length)
-                def _(s=s, way=way, length=length):
-                    lhs = heads_of((1 - 2 * way) * (length - step + 1))
-                    own_term[way, s] = jnp.dot(lhs, columns(s), preferred_element_type=F32)
-
-    def out_columns(s):
-        return pl.ds(pl.multiple_of(x * quarter + s * SUB, 128), SUB)
-
-    def reduce_step(step, carry):
-        for s in range(subs):
-            for way in (0, 1):
-                length = length_of(way, s)
-                z_next = z_down if way else z_up
-                slot = 2 * step - 2 + way
-
-                @pl.when(step <= length)
-                def _(s=s, way=way, z_next=z_next, slot=slot, length=length):
-                    @pl.when(step > 1)
-                    def _():
-                        arrived(rs_recv.at[way, step - 1, s], rs_sem.at[way, step - 1, s])
-
-                    term = own_term[way, s] + rs_recv[way, step - 1, s].reshape(
-                        block, SUB
-                    ).astype(F32)
-                    rs_send[slot, s] = term.astype(BF).reshape(NX, rows, SUB)
-
-                    @pl.when(step < length)
-                    def _():
-                        remote(
-                            rs_send.at[slot, s],
-                            rs_recv.at[way, step, s],
-                            send_sem.at[18],
-                            rs_sem.at[way, step, s],
-                            tensor_1=z_next,
-                        ).start()
-
-                    @pl.when(step == length)
-                    def _():
-                        for d in range(NX):
-                            remote(
-                                rs_send.at[slot, s, xs[d]],
-                                out.at[1 + way, :, out_columns(s)],
-                                send_sem.at[18],
-                                fin_sem.at[1 + way, d, s],
-                                tensor_0=xs[d],
-                                tensor_1=z_next,
-                            ).start()
-
-        @pl.when(step < turns)
-        def _():
-            own_terms(step + 1)
-
+        if b + 1 < NX:
+            att_pass(b + 1)
+        ready(b)
+        for back in range(b + 1):
+            reduce_step(b - back, 1 + back)
+    for d in (1, 2, 3):
+        remote(
+            fin.at[xs[d]],
+            out.at[0, :, my_columns],
+            send_sem.at[19],
+            fin_sem.at[0, d],
+            tensor_0=xs[d],
+        ).start()
+    pltpu.make_async_copy(fin.at[x], out.at[0, :, my_columns], fin_sem.at[0, 0]).start()
+
+    def reduce_round(step, carry):
+        for b in reversed(range(NX)):
+            reduce_step(b, step + NX - 1 - b)
         return carry
 
-    own_terms(1)
-    lax.fori_loop(1, turns + 1, reduce_step, 0)
-    own = heads_of(0)
-    for s in range(subs):
-        term = jnp.dot(own, columns(s), preferred_element_type=F32)
-        fin[s] = term.astype(BF).reshape(NX, rows, SUB)
-        for d in (1, 2, 3):
-            remote(
-                fin.at[s, xs[d]],
-                out.at[0, :, out_columns(s)],
-                send_sem.at[19],
-                fin_sem.at[0, d, s],
-                tensor_0=xs[d],
-            ).start()
-        pltpu.make_async_copy(
-            fin.at[s, x], out.at[0, :, out_columns(s)], fin_sem.at[0, 0, s]
-        ).start()
+    lax.fori_loop(2, turns + 1, reduce_round, 0)
 
     n_ring = turns * 2 - 1
     arrived(x_wide.at[pl.ds(0, 3), :, 0], send_sem.at[0])
@@ -591,12 +581,11 @@
     arrived(att.at[0], send_sem.at[15])
     arrived(att.at[0, near], send_sem.at[16])
     arrived(att.at[0, far], send_sem.at[17])
-    for s in range(subs):
-        for d in range(NX):
-            for piece in range(3):
-                arrived(fin.at[s, x], fin_sem.at[piece, d, s])
-    arrived(rs_send.at[pl.ds(0, n_ring)], send_sem.at[18])
-    arrived(fin.at[:, pl.ds(0, 3)], send_sem.at[19])
+    for d in range(NX):
+        for piece in range(3):
+            arrived(fin.at[0], fin_sem.at[piece, d])
+    arrived(rs_send.at[pl.ds(0, NX * n_ring)], send_sem.at[18])
+    arrived(fin.at[pl.ds(0, 3)], send_sem.at[19])
 
 
 def body(hidden_in, first_values, qkv_weight, out_weight, mix_table, mix_index, lengths, *, nz):
@@ -631,10 +620,10 @@
         pltpu.VMEM((NX, nz, rows, hs), BF),
         pltpu.VMEM((NX, nz, rows, hs), BF),
         pltpu.VMEM((NX, nz, NX, rows, hs), BF),
-        pltpu.VMEM((2 * turns, subs, NX, rows, SUB), BF),
-        pltpu.VMEM((2, turns, subs, NX, rows, SUB), BF),
-        pltpu.VMEM((2, subs, block, SUB), F32),
-        pltpu.VMEM((subs, NX, rows, SUB), BF),
+        pltpu.VMEM((NX * 2 * turns, rows, quarter), BF),
+        pltpu.VMEM((NX * 2 * turns, rows, quarter), BF),
+        pltpu.VMEM((NX, nz, rows, quarter), F32),
+        pltpu.VMEM((NX, rows, quarter), BF),
         dma((4,)),
         dma((20,)),
         dma((x_subs + z_subs,)),
@@ -647,8 +636,8 @@
         dma((nz,)),
         dma((nz,)),
         dma((4, NX)),
-        dma((2, turns, subs)),
-        dma((3, NX, subs)),
+        dma((NX * 2 * turns,)),
+        dma((3, NX)),
     ]
     result = pl.pallas_call(
         functools.partial(kernel, nz),

time: 137 us -> 137 us (level)
  no operation moved by 1% of the time
where the time goes in v6:
time: 137 us; the launch traced here: 135 us
  Pallas kernels  132 us (96%)
  other arithmetic  1.8 us (1%)
    pallas_call x1, Pallas kernels, body(): pl.pallas_call(functools.partial(kernel, nz), out_shape=jax.ShapeDtypeStr...  132 us

profile of v6, /device:TPU:40, one launch (start us, length us, event | category | flops | bytes accessed | tf_op | source)
XLA Modules:
  0.0 135.5 jit_solution(15962441696892832090)
XLA Ops:
  1.3 132.4 %shard_map.73 = bf16[3,16,5120]{2,1,0:T(8,128)(2,1)} custom-call(bf16[16,5120]{1,0:T(8,128)(2,1)} %bitcast.6, bf16[16,8192]{1,0:T(8,128)(2,1)} %bitcast.5, bf16[3,5120,128]{2,1,0:T(8,128)(2,1)} %bitcast.4, bf16[128,5120]{1,0:T(8,128)(2,1)} %w_out.1, f32[2,8]{1,0:T(2,128)} %bitcast.7, s32[1]{0:T(128)S(6)} %copy.8.mix_index, s32[1]{0:T(128)S(6)} %copy.9.lengths), custom_call_target="tpu_custom_call" | custom-call | tf_op jit(solution)/shard_map/pallas_call | solution.py:642
  133.7 1.8 %add_convert_fusion = bf16[1,16,5120]{2,1,0:T(8,128)(2,1)} fusion(bf16[3,16,5120]{2,1,0:T(8,128)(2,1)} %shard_map.73), kind=kLoop, calls=%fused_computation | loop fusion | flops 491520 | bytes 655360 | tf_op jit(solution)/shard_map/convert_element_type | solution.py:661

commit v7 on v6

--- a/solution.py
+++ b/solution.py
@@ -129,7 +129,7 @@
                 hid.at[:, x_columns(to_half, s)],
                 x_wide.at[0, s, x],
                 send_sem.at[0],
-                hid_sem.at[d, s],
+                hid_sem.at[d],
                 tensor_0=to,
             ).start()
 
@@ -138,27 +138,55 @@
             hid.at[:, z_columns(theirs, s)],
             z_part.at[0, s, x],
             send_sem.at[1],
-            hid_sem.at[0, s],
+            hid_sem.at[0],
             tensor_0=pair,
         ).start()
     hidden_out(1, pair, theirs)
     hidden_out(2, other, mine)
     hidden_out(3, xs[2], theirs)
-    own_hidden = []
     for s in range(z_subs):
-        own_hidden.append(
-            pltpu.make_async_copy(
-                hid.at[:, z_columns(mine, s)], z_part.at[0, s, x], own_sem.at[s]
-            )
-        )
+        pltpu.make_async_copy(
+            hid.at[:, z_columns(mine, s)], z_part.at[0, s, x], own_sem.at[0]
+        ).start()
     for s in range(x_subs):
-        own_hidden.append(
-            pltpu.make_async_copy(
-                hid.at[:, x_columns(mine, s)], x_wide.at[0, s, x], own_sem.at[z_subs + s]
-            )
-        )
-    for copy in own_hidden:
-        copy.start()
+        pltpu.make_async_copy(
+            hid.at[:, x_columns(mine, s)], x_wide.at[0, s, x], own_sem.at[1]
+        ).start()
+
+    flows = [(0, s, min(2, x_subs - s)) for s in range(0, x_subs, 2)]
+    flows += [(1, s, 1) for s in range(z_subs)]
+
+    def longer(way, n):
+        return turns if (n % 2 == 0) == (way == 0) else turns - 1
+
+    def part(n, place):
+        kind, s, count = flows[n]
+        if kind == 0:
+            return x_wide.at[place, pl.ds(s, count)]
+        return z_part.at[place, s, stripes]
+
+    def ring_send(n, way, step, source, target):
+        remote(
+            source,
+            target,
+            send_sem.at[3 if flows[n][0] == 0 else 5],
+            ag_sem.at[way, step - 1, n],
+            tensor_1=z_down if way else z_up,
+        ).start()
+
+    def other_send(place, s, source, target):
+        remote(source, target, send_sem.at[6], oz_sem.at[place], tensor_0=other).start()
+
+    for n, (kind, first, count) in enumerate(flows):
+        for s in range(first, first + count):
+            for way in (0, 1):
+                target = 1 if way else nz - 1
+                if kind == 0:
+                    ring_send(n, way, 1, hid.at[:, x_columns(mine, s)], x_wide.at[target, s, x])
+                else:
+                    ring_send(n, way, 1, hid.at[:, z_columns(mine, s)], z_part.at[target, s, x])
+            if kind == 1:
+                other_send(0, s, hid.at[:, z_columns(mine, s)], z_part.at[0, s, x])
 
     def stage_firsts(head, carry):
         away = lax.rem(head - z + nz, nz)
@@ -177,7 +205,7 @@
             fv_stage.at[d - 1],
             fv_own.at[:, x],
             send_sem.at[2],
-            fx_sem.at[d],
+            fx_sem.at[0],
             tensor_0=xs[d],
         ).start()
 
@@ -198,14 +226,14 @@
             pltpu.make_async_copy(
                 w_qkv.at[p, pl.ds(pl.multiple_of(mine * halves, 128), halves)],
                 w2.at[:, pl.ds(p * hs, hs)],
-                local_sem.at[p],
+                local_sem.at[0],
             )
         )
     own_weights.append(
         pltpu.make_async_copy(
             w_out.at[:, pl.ds(pl.multiple_of(x * quarter, 128), quarter)],
             wo2.at[pl.ds(0, hs)],
-            local_sem.at[3],
+            local_sem.at[1],
         )
     )
     for copy in own_weights:
@@ -217,75 +245,36 @@
         return pl.ds(pl.multiple_of(to * quarter + core * half, 128), half)
 
     def wo_piece(r):
-        return wo2.at[pl.ds(r * hs, hs), pl.ds(my_half, half)]
+        return wo2.at[pl.ds(pl.multiple_of(r * hs, hs), hs), pl.ds(my_half, half)]
+
+    from_pair, from_other = 1 + 2 * odd, 3 - 2 * odd
 
     def out_weights_send():
         remote(
-            w_out.at[:, wo_columns(xs[2])], wo_relay, send_sem.at[11], wo_sem.at[0], tensor_0=x_way
-        ).start()
-        for d, r, sem in ((1, 3, 1), (3, 1, 2)):
-            remote(
-                w_out.at[:, wo_columns(xs[d])],
-                wo_piece(r),
-                send_sem.at[11],
-                wo_sem.at[sem],
-                tensor_0=xs[d],
-            ).start()
-
-    def out_to_sibling(r):
-        remote(
-            wo_piece(r), wo_piece(r), send_sem.at[12], wo_sem.at[3 + r], dp=1 - core
-        ).start()
-
-    def out_weights_relay():
+            w_out.at[:, wo_columns(pair)], wo_piece(from_other), send_sem.at[11], wo_sem.at[1], tensor_0=pair
+        ).start()
+        remote(
+            w_out.at[:, wo_columns(xs[2])], wo_relay, send_sem.at[11], wo_sem.at[0], tensor_0=pair
+        ).start()
+
+    def out_weights_late():
+        remote(
+            w_out.at[:, wo_columns(other)], wo_piece(from_pair), send_sem.at[11], wo_sem.at[2], tensor_0=other
+        ).start()
         arrived(wo_relay, wo_sem.at[0])
-        remote(wo_relay, wo_piece(2), send_sem.at[13], wo_sem.at[3], tensor_0=x_way).start()
-
-    def out_weights_direct():
-        for r, sem in ((3, 1), (1, 2)):
-            arrived(wo_piece(r), wo_sem.at[sem])
-            out_to_sibling(r)
-
-    def out_weights_last():
-        arrived(wo_piece(2), wo_sem.at[3])
-        out_to_sibling(2)
+        remote(wo_relay, wo_piece(2), send_sem.at[13], wo_sem.at[3], tensor_0=other).start()
+
+    def out_to_sibling(r, sem):
+        arrived(wo_piece(r), wo_sem.at[sem])
+        remote(
+            wo_piece(r), wo_piece(r), send_sem.at[12], wo_sem.at[3 + sem], dp=1 - core
+        ).start()
 
     def out_weights_wait():
-        other = pl.multiple_of((1 - core) * half, 128)
-        for r in (1, 2, 3):
-            arrived(wo2.at[pl.ds(r * hs, hs), pl.ds(other, half)], wo_sem.at[3 + r])
+        for sem in (1, 2, 3):
+            arrived(wo_piece(0), wo_sem.at[3 + sem])
 
     out_weights_send()
-
-    flows = [(0, s) for s in range(x_subs)] + [(1, s) for s in range(z_subs)]
-
-    def longer(way, n):
-        return turns if (n % 2 == 0) == (way == 0) else turns - 1
-
-    def part(n, place):
-        kind, s = flows[n]
-        return x_wide.at[place, s] if kind == 0 else z_part.at[place, s, stripes]
-
-    def ring_send(n, way, step):
-        source, target = (step - 1, step) if way else ((nz - step + 1) % nz, nz - step)
-        remote(
-            part(n, source),
-            part(n, target),
-            send_sem.at[3 if flows[n][0] == 0 else 5],
-            ag_sem.at[way, step - 1, n],
-            tensor_1=z_down if way else z_up,
-        ).start()
-
-    def to_other(n, place):
-        kind, s = flows[n]
-        if kind == 1:
-            remote(
-                z_part.at[place, s, stripes],
-                z_part.at[place, s, stripes],
-                send_sem.at[6],
-                oz_sem.at[place, s],
-                tensor_0=other,
-            ).start()
 
     def gather_step(step):
         for n in range(len(flows)):
@@ -294,8 +283,10 @@
                     place = step if way else nz - step
                     arrived(part(n, place), ag_sem.at[way, step - 1, n])
                     if step + 1 <= longer(way, n):
-                        ring_send(n, way, step + 1)
-                    to_other(n, place)
+                        onward = step + 1 if way else nz - step - 1
+                        ring_send(n, way, step + 1, part(n, place), part(n, onward))
+                    if flows[n][0] == 1:
+                        other_send(place, flows[n][1], part(n, place), part(n, place))
 
     def weights_step(p):
         here = w2.at[pl.ds(my_share, share), pl.ds((3 + p) * hs, hs)]
@@ -307,34 +298,39 @@
             arrived(
                 w2.at[pl.ds(sibling_share, share), pl.ds((3 + p) * hs, hs)], w_sem.at[1, p]
             )
-        for copy in own_weights:
-            copy.wait()
+        arrived(w2.at[:, pl.ds(0, 3 * hs)], local_sem.at[0])
+        arrived(wo2.at[pl.ds(0, hs)], local_sem.at[1])
 
     def firsts_step(step):
         if step == 1:
-            for d in (1, 2, 3):
-                arrived(fv_stage.at[d - 1], fx_sem.at[d])
+            arrived(fv_stage, fx_sem.at[0])
         for away in sorted({step, nz - step}):
             remote(
                 fv_own.at[away],
                 fv_in.at[nz - away],
                 send_sem.at[8],
-                fz_sem.at[nz - away],
+                fz_sem.at[0],
                 tensor_1=lax.rem(z + away, nz),
             ).start()
 
-    for copy in own_hidden:
-        copy.wait()
-    for s in range(z_subs):
-        arrived(z_part.at[0, s, pair], hid_sem.at[0, s])
-        ring_send(x_subs + s, 0, 1)
-        ring_send(x_subs + s, 1, 1)
-        to_other(x_subs + s, 0)
-    for s in range(x_subs):
-        for d in (1, 2, 3):
-            arrived(x_wide.at[0, s, x], hid_sem.at[d, s])
-        ring_send(s, 0, 1)
-        ring_send(s, 1, 1)
+    arrived(z_part.at[0, :, x], hid_sem.at[0])
+    for n, (kind, first, count) in enumerate(flows):
+        if kind == 1:
+            piece = z_part.at[0, first, pair]
+            ring_send(n, 0, 1, piece, z_part.at[nz - 1, first, pair])
+            ring_send(n, 1, 1, piece, z_part.at[1, first, pair])
+            other_send(0, first, piece, piece)
+    for d in (1, 2, 3):
+        arrived(x_wide.at[0, :, x], hid_sem.at[d])
+    for n, (kind, first, count) in enumerate(flows):
+        if kind == 0:
+            for d in (1, 2, 3):
+                at = pl.ds(first, count)
+                piece = x_wide.at[0, at, xs[d]]
+                ring_send(n, 0, 1, piece, x_wide.at[nz - 1, at, xs[d]])
+                ring_send(n, 1, 1, piece, x_wide.at[1, at, xs[d]])
+    arrived(z_part.at[0, :, x], own_sem.at[0])
+    arrived(x_wide.at[0, :, x], own_sem.at[1])
     early = max(turns - 3, 0)
     weights_after = {2: (0,), 3: (1,), 4: (2,)}
     for step in range(1, early + 1):
@@ -353,8 +349,7 @@
 
     def project(i):
         place = place_of(i)
-        for s in range(z_subs):
-            arrived(z_part.at[place, s, other_stripes], oz_sem.at[place, s])
+        arrived(z_part.at[place, :, other_stripes], oz_sem.at[place])
         lhs = jnp.concatenate(
             [x_wide[place, s].reshape(block, SUB) for s in range(x_subs)]
             + [z_part[place, s].reshape(block, z_wide) for s in range(z_subs)],
@@ -389,9 +384,8 @@
                 min(at, 2 * step - 1),
                 *(functools.partial(firsts_step, away) for away in range(1, turns + 1)),
             )
-    at_trip(4, out_weights_relay)
-    at_trip(6, out_weights_direct)
-    at_trip(12, out_weights_last)
+    at_trip(12, out_weights_late)
+    at_trip(12, functools.partial(out_to_sibling, from_pair, 1))
 
     def trip(i, carry):
         for at, steps in late.items():
@@ -412,8 +406,6 @@
         return carry
 
     lax.fori_loop(0, trips, trip, 0)
-    out_weights_wait()
-
     row = mix_index[0]
     weight_now = mix_table[0, row]
     weight_first = mix_table[1, row]
@@ -423,8 +415,8 @@
         v_buf[:, origin] = (weight_now * now + weight_first * first.astype(F32)).astype(BF)
 
     mix(z, fv_own[0])
+    arrived(fv_in.at[pl.ds(1, nz - 1)], fz_sem.at[0])
     for away in range(1, nz):
-        arrived(fv_in.at[away], fz_sem.at[away])
         mix(lax.rem(z + away, nz), fv_in[away])
 
     scale = 1.0 / math.sqrt(hs)
@@ -473,7 +465,7 @@
         ).start()
         arrived(att.at[1, :, b], att_sem.at[1, b])
         remote(
-            att.at[1, far, b], att.at[2, far, b], send_sem.at[17], att_sem.at[3, b], tensor_0=xs[3]
+            att.at[1, far, b], att.at[2, far, b], send_sem.at[17], att_sem.at[2, b], tensor_0=xs[3]
         ).start()
 
     my_columns = pl.ds(pl.multiple_of(x * quarter, 128), quarter)
@@ -482,8 +474,7 @@
         return turns if (b % 2 == 0) == (way == 0) else turns - 1
 
     def ready(b):
-        arrived(att.at[2, near, b], att_sem.at[2, b])
-        arrived(att.at[2, far, b], att_sem.at[3, b])
+        arrived(att.at[2, :, b], att_sem.at[2, b])
         lhs = jnp.concatenate([att[r, :, b].reshape(stripe, hs) for r in range(NX)], axis=1)
         for s in range(subs):
             column = slice(s * SUB, (s + 1) * SUB)
@@ -519,7 +510,7 @@
                         rs_send.at[slot - 1],
                         out.at[1 + way, :, my_columns],
                         send_sem.at[18],
-                        fin_sem.at[1 + way, lax.rem(b - x + NX, NX)],
+                        fin_sem.at[0],
                         tensor_0=jnp.int32(b),
                         tensor_1=z_next,
                     ).start()
@@ -539,7 +530,10 @@
     for b in range(NX):
         attend(b)
         att_send(b)
+    out_to_sibling(from_other, 2)
+    out_to_sibling(2, 3)
     att_pass(0)
+    out_weights_wait()
     for b in range(NX):
         if b + 1 < NX:
             att_pass(b + 1)
@@ -551,10 +545,10 @@
             fin.at[xs[d]],
             out.at[0, :, my_columns],
             send_sem.at[19],
-            fin_sem.at[0, d],
+            fin_sem.at[0],
             tensor_0=xs[d],
         ).start()
-    pltpu.make_async_copy(fin.at[x], out.at[0, :, my_columns], fin_sem.at[0, 0]).start()
+    pltpu.make_async_copy(fin.at[x], out.at[0, :, my_columns], fin_sem.at[0]).start()
 
     def reduce_round(step, carry):
         for b in reversed(range(NX)):
@@ -581,9 +575,7 @@
     arrived(att.at[0], send_sem.at[15])
     arrived(att.at[0, near], send_sem.at[16])
     arrived(att.at[0, far], send_sem.at[17])
-    for d in range(NX):
-        for piece in range(3):
-            arrived(fin.at[0], fin_sem.at[piece, d])
+    arrived(rs_recv.at[pl.ds(0, 3 * NX)], fin_sem.at[0])
     arrived(rs_send.at[pl.ds(0, NX * n_ring)], send_sem.at[18])
     arrived(fin.at[pl.ds(0, 3)], send_sem.at[19])
 
@@ -595,7 +587,7 @@
     half = quarter // 2
     halves = model // 2
     subs = quarter // SUB
-    x_subs = max(1, halves * 4 // 10 // SUB)
+    x_subs = max(1, halves * 3 // 10 // SUB)
     z_subs = 2
     z_wide = (halves - x_subs * SUB) // z_subs
     turns = nz // 2
@@ -624,20 +616,20 @@
         pltpu.VMEM((NX * 2 * turns, rows, quarter), BF),
         pltpu.VMEM((NX, nz, rows, quarter), F32),
         pltpu.VMEM((NX, rows, quarter), BF),
-        dma((4,)),
+        dma((2,)),
         dma((20,)),
-        dma((x_subs + z_subs,)),
-        dma((NX, x_subs + z_subs)),
-        dma((2, turns, x_subs + z_subs)),
-        dma((nz, z_subs)),
+        dma((2,)),
+        dma((NX,)),
+        dma((2, turns, (x_subs + 1) // 2 + z_subs)),
+        dma((nz,)),
         dma((2, 3)),
         dma((7,)),
-        dma((NX,)),
+        dma((1,)),
+        dma((1,)),
         dma((nz,)),
-        dma((nz,)),
-        dma((4, NX)),
+        dma((3, NX)),
         dma((NX * 2 * turns,)),
-        dma((3, NX)),
+        dma((1,)),
     ]
     result = pl.pallas_call(
         functools.partial(kernel, nz),

time: 137 us -> 135 us (0.985)
  Pallas kernels: 132 us -> 130 us
    pallas_call x1, Pallas kernels: 132 us -> 130 us  [body(): pl.pallas_call(functools.partial(kernel, nz), out_shape=jax.ShapeDtypeStr...]
where the time goes in v7:
time: 135 us; the launch traced here: 133 us
  Pallas kernels  130 us (96%)
  other arithmetic  1.8 us (1%)
    pallas_call x1, Pallas kernels, body(): pl.pallas_call(functools.partial(kernel, nz), out_shape=jax.ShapeDtypeStr...  130 us

profile of v7, /device:TPU:40, one launch (start us, length us, event | category | flops | bytes accessed | tf_op | source)
XLA Modules:
  0.0 133.3 jit_solution(10096652629512895494)
XLA Ops:
  1.3 130.2 %shard_map.73 = bf16[3,16,5120]{2,1,0:T(8,128)(2,1)} custom-call(bf16[16,5120]{1,0:T(8,128)(2,1)} %bitcast.6, bf16[16,8192]{1,0:T(8,128)(2,1)} %bitcast.5, bf16[3,5120,128]{2,1,0:T(8,128)(2,1)} %bitcast.4, bf16[128,5120]{1,0:T(8,128)(2,1)} %w_out.1, f32[2,8]{1,0:T(2,128)} %bitcast.7, s32[1]{0:T(128)S(6)} %copy.8.mix_index, s32[1]{0:T(128)S(6)} %copy.9.lengths), custom_call_target="tpu_custom_call" | custom-call | tf_op jit(solution)/shard_map/pallas_call | solution.py:634
  131.5 1.8 %add_convert_fusion = bf16[1,16,5120]{2,1,0:T(8,128)(2,1)} fusion(bf16[3,16,5120]{2,1,0:T(8,128)(2,1)} %shard_map.73), kind=kLoop, calls=%fused_computation | loop fusion | flops 491520 | bytes 655360 | tf_op jit(solution)/shard_map/convert_element_type | solution.py:653

commit v8 on v7

--- a/solution.py
+++ b/solution.py
@@ -532,14 +532,12 @@
         att_send(b)
     out_to_sibling(from_other, 2)
     out_to_sibling(2, 3)
-    att_pass(0)
+    for b in range(NX):
+        att_pass(b)
     out_weights_wait()
     for b in range(NX):
-        if b + 1 < NX:
-            att_pass(b + 1)
         ready(b)
-        for back in range(b + 1):
-            reduce_step(b - back, 1 + back)
+        reduce_step(b, 1)
     for d in (1, 2, 3):
         remote(
             fin.at[xs[d]],
@@ -551,8 +549,8 @@
     pltpu.make_async_copy(fin.at[x], out.at[0, :, my_columns], fin_sem.at[0]).start()
 
     def reduce_round(step, carry):
-        for b in reversed(range(NX)):
-            reduce_step(b, step + NX - 1 - b)
+        for b in range(NX):
+            reduce_step(b, step)
         return carry
 
     lax.fori_loop(2, turns + 1, reduce_round, 0)

time: 135 us -> 131 us (0.970)
  Pallas kernels: 130 us -> 126 us
    pallas_call x1, Pallas kernels: 130 us -> 126 us  [body(): pl.pallas_call(functools.partial(kernel, nz), out_shape=jax.ShapeDtypeStr...]
where the time goes in v8:
time: 131 us; the launch traced here: 129 us
  Pallas kernels  126 us (96%)
  other arithmetic  1.8 us (1%)
    pallas_call x1, Pallas kernels, body(): pl.pallas_call(functools.partial(kernel, nz), out_shape=jax.ShapeDtypeStr...  126 us

profile of v8, /device:TPU:40, one launch (start us, length us, event | category | flops | bytes accessed | tf_op | source)
XLA Modules:
  0.0 129.5 jit_solution(12434616329715481270)
XLA Ops:
  1.3 126.4 %shard_map.73 = bf16[3,16,5120]{2,1,0:T(8,128)(2,1)} custom-call(bf16[16,5120]{1,0:T(8,128)(2,1)} %bitcast.6, bf16[16,8192]{1,0:T(8,128)(2,1)} %bitcast.5, bf16[3,5120,128]{2,1,0:T(8,128)(2,1)} %bitcast.4, bf16[128,5120]{1,0:T(8,128)(2,1)} %w_out.1, f32[2,8]{1,0:T(2,128)} %bitcast.7, s32[1]{0:T(128)S(6)} %copy.8.mix_index, s32[1]{0:T(128)S(6)} %copy.9.lengths), custom_call_target="tpu_custom_call" | custom-call | tf_op jit(solution)/shard_map/pallas_call | solution.py:632
  127.7 1.8 %add_convert_fusion = bf16[1,16,5120]{2,1,0:T(8,128)(2,1)} fusion(bf16[3,16,5120]{2,1,0:T(8,128)(2,1)} %shard_map.73), kind=kLoop, calls=%fused_computation | loop fusion | flops 491520 | bytes 655360 | tf_op jit(solution)/shard_map/convert_element_type | solution.py:651

commit v9 on v8

--- a/solution.py
+++ b/solution.py
@@ -20,14 +20,20 @@
 
 def kernel(
     nz,
+    hid_in,
+    firsts_in,
+    w_qkv,
+    w_out,
+    table_in,
+    index_in,
+    lengths_in,
+    out,
     hid,
     firsts,
-    w_qkv,
-    w_out,
     mix_table,
     mix_index,
     lengths,
-    out,
+    load_sem,
     x_wide,
     z_part,
     w2,
@@ -108,7 +114,22 @@
         pl.semaphore_signal(
             barrier, inc=1, device_id=partner, device_id_type=pl.DeviceIdType.MESH
         )
+    loads = [
+        pltpu.make_async_copy(source, target, load_sem.at[n])
+        for n, (source, target) in enumerate(
+            (
+                (hid_in, hid),
+                (firsts_in, firsts),
+                (table_in, mix_table),
+                (index_in, mix_index),
+                (lengths_in, lengths),
+            )
+        )
+    ]
+    for load in loads:
+        load.start()
     pl.semaphore_wait(barrier, len(partners))
+    loads[0].wait()
 
     def half_of(at):
         return lax.rem((at + 1) // 2, 2)
@@ -199,6 +220,7 @@
                 fv_stage[d - 1, away] = piece
         return carry
 
+    loads[1].wait()
     lax.fori_loop(0, nz, stage_firsts, 0)
     for d in (1, 2, 3):
         remote(
@@ -406,6 +428,8 @@
         return carry
 
     lax.fori_loop(0, trips, trip, 0)
+    for load in loads[2:]:
+        load.wait()
     row = mix_index[0]
     weight_now = mix_table[0, row]
     weight_first = mix_table[1, row]
@@ -590,11 +614,15 @@
     z_wide = (halves - x_subs * SUB) // z_subs
     turns = nz // 2
     block = NX * rows
-    vmem = pl.BlockSpec(memory_space=pltpu.VMEM)
-    smem = pl.BlockSpec(memory_space=pltpu.SMEM)
     anywhere = pl.BlockSpec(memory_space=pl.ANY)
     dma = pltpu.SemaphoreType.DMA
     scratch = [
+        pltpu.VMEM((rows, model), BF),
+        pltpu.VMEM(first_values.shape[1:], BF),
+        pltpu.SMEM(mix_table.shape[::-1], F32),
+        pltpu.SMEM(mix_index.shape, jnp.int32),
+        pltpu.SMEM(lengths.shape, jnp.int32),
+        dma((5,)),
         pltpu.VMEM((nz, x_subs, NX, rows, SUB), BF),
         pltpu.VMEM((nz, z_subs, NX, rows, z_wide), BF),
         pltpu.VMEM((halves, 2 * 3 * hs), BF),
@@ -632,7 +660,7 @@
     result = pl.pallas_call(
         functools.partial(kernel, nz),
         out_shape=jax.ShapeDtypeStruct((3, rows, model), BF),
-        in_specs=[vmem, vmem, anywhere, anywhere, smem, smem, smem],
+        in_specs=[anywhere] * 7,
         out_specs=anywhere,
         scratch_shapes=scratch,
         compiler_params=pltpu.CompilerParams(

time: 131 us -> 130 us (level)
  no operation moved by 1% of the time
where the time goes in v9:
time: 130 us; the launch traced here: 129 us
  Pallas kernels  126 us (97%)
  other arithmetic  1.8 us (1%)
  between operations  1.3 us (1%)
    pallas_call x1, Pallas kernels, body(): pl.pallas_call(functools.partial(kernel, nz), out_shape=jax.ShapeDtypeStr...  126 us

profile of v9, /device:TPU:40, one launch (start us, length us, event | category | flops | bytes accessed | tf_op | source)
XLA Modules:
  0.0 128.9 jit_solution(16238661885872337399)
XLA Ops:
  1.3 125.8 %shard_map.73 = bf16[3,16,5120]{2,1,0:T(8,128)(2,1)} custom-call(bf16[16,5120]{1,0:T(8,128)(2,1)} %bitcast.6, bf16[16,8192]{1,0:T(8,128)(2,1)} %bitcast.5, bf16[3,5120,128]{2,1,0:T(8,128)(2,1)} %bitcast.4, bf16[128,5120]{1,0:T(8,128)(2,1)} %w_out.1, f32[2,8]{1,0:T(2,128)} %bitcast.7, s32[1]{0:T(128)S(6)} %copy.8.index_in, s32[1]{0:T(128)S(6)} %copy.9.lengths_in), custom_call_target="tpu_custom_call" | custom-call | tf_op jit(solution)/shard_map/pallas_call | solution.py:660
  127.1 1.8 %add_convert_fusion = bf16[1,16,5120]{2,1,0:T(8,128)(2,1)} fusion(bf16[3,16,5120]{2,1,0:T(8,128)(2,1)} %shard_map.73), kind=kLoop, calls=%fused_computation | loop fusion | flops 491520 | bytes 655360 | tf_op jit(solution)/shard_map/convert_element_type | solution.py:679

commit v10 on v9

--- a/solution.py
+++ b/solution.py
@@ -174,7 +174,7 @@
             hid.at[:, x_columns(mine, s)], x_wide.at[0, s, x], own_sem.at[1]
         ).start()
 
-    flows = [(0, s, min(2, x_subs - s)) for s in range(0, x_subs, 2)]
+    flows = [(0, s, 1) for s in range(x_subs)]
     flows += [(1, s, 1) for s in range(z_subs)]
 
     def longer(way, n):
@@ -646,7 +646,7 @@
         dma((20,)),
         dma((2,)),
         dma((NX,)),
-        dma((2, turns, (x_subs + 1) // 2 + z_subs)),
+        dma((2, turns, x_subs + z_subs)),
         dma((nz,)),
         dma((2, 3)),
         dma((7,)),

time: 130 us -> 130 us (level)
  no operation moved by 1% of the time
where the time goes in v10:
time: 130 us; the launch traced here: 128 us
  Pallas kernels  125 us (96%)
  other arithmetic  1.8 us (1%)
  between operations  1.3 us (1%)
    pallas_call x1, Pallas kernels, body(): pl.pallas_call(functools.partial(kernel, nz), out_shape=jax.ShapeDtypeStr...  125 us

profile of v10, /device:TPU:40, one launch (start us, length us, event | category | flops | bytes accessed | tf_op | source)
XLA Modules:
  0.0 128.2 jit_solution(11546555531051424041)
XLA Ops:
  1.3 125.1 %shard_map.73 = bf16[3,16,5120]{2,1,0:T(8,128)(2,1)} custom-call(bf16[16,5120]{1,0:T(8,128)(2,1)} %bitcast.6, bf16[16,8192]{1,0:T(8,128)(2,1)} %bitcast.5, bf16[3,5120,128]{2,1,0:T(8,128)(2,1)} %bitcast.4, bf16[128,5120]{1,0:T(8,128)(2,1)} %w_out.1, f32[2,8]{1,0:T(2,128)} %bitcast.7, s32[1]{0:T(128)S(6)} %copy.8.index_in, s32[1]{0:T(128)S(6)} %copy.9.lengths_in), custom_call_target="tpu_custom_call" | custom-call | tf_op jit(solution)/shard_map/pallas_call | solution.py:660
  126.4 1.8 %add_convert_fusion = bf16[1,16,5120]{2,1,0:T(8,128)(2,1)} fusion(bf16[3,16,5120]{2,1,0:T(8,128)(2,1)} %shard_map.73), kind=kLoop, calls=%fused_computation | loop fusion | flops 491520 | bytes 655360 | tf_op jit(solution)/shard_map/convert_element_type | solution.py:679
